TPU v7x, 8 devices: a whole 2x2x1 slice. The times are simulated.
8 devices in a mesh: row: 4 (over z, y, x), col: 2 (over core).
Axes of the slice: x: 2, y: 2, z: 1, core: 2. Of those that a mesh axis runs over, the one named last changes fastest.
Arguments:
- v_panels: float32 [16384, 16384], P('row', 'col')
- t_factors: float32 [128, 128, 128], P('col')
- z_vectors: float32 [16384, 1024], P(None, ('col', 'row'))
Outputs:
- output: float32 [16384, 1024], P('row', 'col')
All inputs are finite; a program needn't handle non-finite values.
Results may differ from a plain program's by a relative error of at most 0.001.
Values sent between devices are 32-bit elements.
A program may use at most 1 GiB of HBM per device.

v0:
```python
import jax
import jax.numpy as jnp
from jax import lax
from jax.sharding import PartitionSpec as P, NamedSharding

HIGHEST = lax.Precision.HIGHEST


def solution(mesh):
    col_devs = mesh.shape['col']

    def local_apply(v_loc, t_loc, z_loc):
        panel_width = t_loc.shape[1]
        groups = t_loc.shape[0]
        x_loc = lax.all_to_all(z_loc, 'row', 0, 1, tiled=True)

        def group_step(step_idx, x_cur):
            group_idx = groups - 1 - step_idx
            v_blk = lax.dynamic_slice_in_dim(v_loc, group_idx * panel_width, panel_width, axis=1)
            t_blk = lax.dynamic_index_in_dim(t_loc, group_idx, axis=0, keepdims=False)
            v_group = lax.all_gather(v_blk, 'col', axis=0)
            t_group = lax.all_gather(t_blk, 'col', axis=0)

            def panel_step(pos_idx, x_in):
                col_pos = col_devs - 1 - pos_idx
                v_j = lax.dynamic_index_in_dim(v_group, col_pos, axis=0, keepdims=False)
                t_j = lax.dynamic_index_in_dim(t_group, col_pos, axis=0, keepdims=False)
                w_part = jnp.einsum('na,nk->ak', v_j, x_in, precision=HIGHEST, preferred_element_type=jnp.float32)
                w_full = lax.psum(w_part, 'row')
                y_mat = jnp.dot(t_j, w_full, precision=HIGHEST, preferred_element_type=jnp.float32)
                return x_in - jnp.dot(v_j, y_mat, precision=HIGHEST, preferred_element_type=jnp.float32)

            return lax.fori_loop(0, col_devs, panel_step, x_cur)

        return lax.fori_loop(0, groups, group_step, x_loc)

    return jax.shard_map(local_apply, mesh=mesh,
                         in_specs=(P('row', 'col'), P('col', None, None), P(None, ('col', 'row'))),
                         out_specs=P('row', 'col'), check_vma=False)
```

profile of v0, /device:TPU:0, one launch (start us, length us, event | category | flops | bytes accessed | tf_op | source)
XLA Modules:
  0.0 8122.1 jit_solution(16244227937075425244)
XLA Ops:
  124.1 7991.2 %while.44 = (s32[]{:T(128)}, f32[4096,512]{1,0:T(8,128)}, f32[4096,8192]{1,0:T(8,128)}, f32[64,128,128]{2,1,0:T(8,128)}, s32[]{:T(128)}, /*index=5*/s32[]{:T(128...) while((s32[]{:T(128)}, f32[4096,512]{1,0:T(8,128)}, ...), condition=%wide.region_4.5_spmd, body=%wide.region_0.4_spmd.sunk | while | flops 6545276928 | bytes 55443968 | solution.py:35
  263.6 110.4 %while.45 = (s32[]{:T(128)}, f32[4096,512]{1,0:T(8,128)}, f32[2,4096,128]{2,1,0:T(8,128)}, f32[2,128,128]{2,1,0:T(8,128)S(1)}, s32[]{:T(128)}, /*index=5*/s32[]{:T(128)}, s32[]{:T(128)}) while((s32[]{:T(128)}, f32[4096,512]{1,0:T(8,128)}, f32[2,4096,128]{2,1,0:T(8,128)}, f32[2,128,128]{2,1,0:T(8,128)S(1)}, s32[]{:T(128)}, ...), condition=%wide.region_3.3_spmd, body=%wide.region_1.2_spmd.sunk | while | flops 6545276928 | bytes 32047280 | solution.py:33
  388.5 110.4 %while.45 = (s32[]{:T(128)}, f32[4096,512]{1,0:T(8,128)}, f32[2,4096,128]{2,1,0:T(8,128)}, f32[2,128,128]{2,1,0:T(8,128)S(1)}, s32[]{:T(128)}, /*index=5*/s32[]{:T(128)}, s32[]{:T(128)}) while((s32[]{:T(128)}, f32[4096,512]{1,0:T(8,128)}, f32[2,4096,128]{2,1,0:T(8,128)}, f32[2,128,128]{2,1,0:T(8,128)S(1)}, s32[]{:T(128)}, ...), condition=%wide.region_3.3_spmd, body=%wide.region_1.2_spmd.sunk | while | flops 6545276928 | bytes 32047280 | solution.py:33
  513.3 110.4 %while.45 = (s32[]{:T(128)}, f32[4096,512]{1,0:T(8,128)}, f32[2,4096,128]{2,1,0:T(8,128)}, f32[2,128,128]{2,1,0:T(8,128)S(1)}, s32[]{:T(128)}, /*index=5*/s32[]{:T(128)}, s32[]{:T(128)}) while((s32[]{:T(128)}, f32[4096,512]{1,0:T(8,128)}, f32[2,4096,128]{2,1,0:T(8,128)}, f32[2,128,128]{2,1,0:T(8,128)S(1)}, s32[]{:T(128)}, ...), condition=%wide.region_3.3_spmd, body=%wide.region_1.2_spmd.sunk | while | flops 6545276928 | bytes 32047280 | solution.py:33
  638.2 110.4 %while.45 = (s32[]{:T(128)}, f32[4096,512]{1,0:T(8,128)}, f32[2,4096,128]{2,1,0:T(8,128)}, f32[2,128,128]{2,1,0:T(8,128)S(1)}, s32[]{:T(128)}, /*index=5*/s32[]{:T(128)}, s32[]{:T(128)}) while((s32[]{:T(128)}, f32[4096,512]{1,0:T(8,128)}, f32[2,4096,128]{2,1,0:T(8,128)}, f32[2,128,128]{2,1,0:T(8,128)S(1)}, s32[]{:T(128)}, ...), condition=%wide.region_3.3_spmd, body=%wide.region_1.2_spmd.sunk | while | flops 6545276928 | bytes 32047280 | solution.py:33
  763.0 110.4 %while.45 = (s32[]{:T(128)}, f32[4096,512]{1,0:T(8,128)}, f32[2,4096,128]{2,1,0:T(8,128)}, f32[2,128,128]{2,1,0:T(8,128)S(1)}, s32[]{:T(128)}, /*index=5*/s32[]{:T(128)}, s32[]{:T(128)}) while((s32[]{:T(128)}, f32[4096,512]{1,0:T(8,128)}, f32[2,4096,128]{2,1,0:T(8,128)}, f32[2,128,128]{2,1,0:T(8,128)S(1)}, s32[]{:T(128)}, ...), condition=%wide.region_3.3_spmd, body=%wide.region_1.2_spmd.sunk | while | flops 6545276928 | bytes 32047280 | solution.py:33
  887.9 110.4 %while.45 = (s32[]{:T(128)}, f32[4096,512]{1,0:T(8,128)}, f32[2,4096,128]{2,1,0:T(8,128)}, f32[2,128,128]{2,1,0:T(8,128)S(1)}, s32[]{:T(128)}, /*index=5*/s32[]{:T(128)}, s32[]{:T(128)}) while((s32[]{:T(128)}, f32[4096,512]{1,0:T(8,128)}, f32[2,4096,128]{2,1,0:T(8,128)}, f32[2,128,128]{2,1,0:T(8,128)S(1)}, s32[]{:T(128)}, ...), condition=%wide.region_3.3_spmd, body=%wide.region_1.2_spmd.sunk | while | flops 6545276928 | bytes 32047280 | solution.py:33
  1012.8 110.4 %while.45 = (s32[]{:T(128)}, f32[4096,512]{1,0:T(8,128)}, f32[2,4096,128]{2,1,0:T(8,128)}, f32[2,128,128]{2,1,0:T(8,128)S(1)}, s32[]{:T(128)}, /*index=5*/s32[]{:T(128)}, s32[]{:T(128)}) while((s32[]{:T(128)}, f32[4096,512]{1,0:T(8,128)}, f32[2,4096,128]{2,1,0:T(8,128)}, f32[2,128,128]{2,1,0:T(8,128)S(1)}, s32[]{:T(128)}, ...), condition=%wide.region_3.3_spmd, body=%wide.region_1.2_spmd.sunk | while | flops 6545276928 | bytes 32047280 | solution.py:33
  1137.6 110.4 %while.45 = (s32[]{:T(128)}, f32[4096,512]{1,0:T(8,128)}, f32[2,4096,128]{2,1,0:T(8,128)}, f32[2,128,128]{2,1,0:T(8,128)S(1)}, s32[]{:T(128)}, /*index=5*/s32[]{:T(128)}, s32[]{:T(128)}) while((s32[]{:T(128)}, f32[4096,512]{1,0:T(8,128)}, f32[2,4096,128]{2,1,0:T(8,128)}, f32[2,128,128]{2,1,0:T(8,128)S(1)}, s32[]{:T(128)}, ...), condition=%wide.region_3.3_spmd, body=%wide.region_1.2_spmd.sunk | while | flops 6545276928 | bytes 32047280 | solution.py:33
  1262.5 110.4 %while.45 = (s32[]{:T(128)}, f32[4096,512]{1,0:T(8,128)}, f32[2,4096,128]{2,1,0:T(8,128)}, f32[2,128,128]{2,1,0:T(8,128)S(1)}, s32[]{:T(128)}, /*index=5*/s32[]{:T(128)}, s32[]{:T(128)}) while((s32[]{:T(128)}, f32[4096,512]{1,0:T(8,128)}, f32[2,4096,128]{2,1,0:T(8,128)}, f32[2,128,128]{2,1,0:T(8,128)S(1)}, s32[]{:T(128)}, ...), condition=%wide.region_3.3_spmd, body=%wide.region_1.2_spmd.sunk | while | flops 6545276928 | bytes 32047280 | solution.py:33
  1387.3 110.4 %while.45 = (s32[]{:T(128)}, f32[4096,512]{1,0:T(8,128)}, f32[2,4096,128]{2,1,0:T(8,128)}, f32[2,128,128]{2,1,0:T(8,128)S(1)}, s32[]{:T(128)}, /*index=5*/s32[]{:T(128)}, s32[]{:T(128)}) while((s32[]{:T(128)}, f32[4096,512]{1,0:T(8,128)}, f32[2,4096,128]{2,1,0:T(8,128)}, f32[2,128,128]{2,1,0:T(8,128)S(1)}, s32[]{:T(128)}, ...), condition=%wide.region_3.3_spmd, body=%wide.region_1.2_spmd.sunk | while | flops 6545276928 | bytes 32047280 | solution.py:33
  1512.2 110.4 %while.45 = (s32[]{:T(128)}, f32[4096,512]{1,0:T(8,128)}, f32[2,4096,128]{2,1,0:T(8,128)}, f32[2,128,128]{2,1,0:T(8,128)S(1)}, s32[]{:T(128)}, /*index=5*/s32[]{:T(128)}, s32[]{:T(128)}) while((s32[]{:T(128)}, f32[4096,512]{1,0:T(8,128)}, f32[2,4096,128]{2,1,0:T(8,128)}, f32[2,128,128]{2,1,0:T(8,128)S(1)}, s32[]{:T(128)}, ...), condition=%wide.region_3.3_spmd, body=%wide.region_1.2_spmd.sunk | while | flops 6545276928 | bytes 32047280 | solution.py:33
  1637.0 110.4 %while.45 = (s32[]{:T(128)}, f32[4096,512]{1,0:T(8,128)}, f32[2,4096,128]{2,1,0:T(8,128)}, f32[2,128,128]{2,1,0:T(8,128)S(1)}, s32[]{:T(128)}, /*index=5*/s32[]{:T(128)}, s32[]{:T(128)}) while((s32[]{:T(128)}, f32[4096,512]{1,0:T(8,128)}, f32[2,4096,128]{2,1,0:T(8,128)}, f32[2,128,128]{2,1,0:T(8,128)S(1)}, s32[]{:T(128)}, ...), condition=%wide.region_3.3_spmd, body=%wide.region_1.2_spmd.sunk | while | flops 6545276928 | bytes 32047280 | solution.py:33
  1761.9 110.4 %while.45 = (s32[]{:T(128)}, f32[4096,512]{1,0:T(8,128)}, f32[2,4096,128]{2,1,0:T(8,128)}, f32[2,128,128]{2,1,0:T(8,128)S(1)}, s32[]{:T(128)}, /*index=5*/s32[]{:T(128)}, s32[]{:T(128)}) while((s32[]{:T(128)}, f32[4096,512]{1,0:T(8,128)}, f32[2,4096,128]{2,1,0:T(8,128)}, f32[2,128,128]{2,1,0:T(8,128)S(1)}, s32[]{:T(128)}, ...), condition=%wide.region_3.3_spmd, body=%wide.region_1.2_spmd.sunk | while | flops 6545276928 | bytes 32047280 | solution.py:33
  1886.8 110.4 %while.45 = (s32[]{:T(128)}, f32[4096,512]{1,0:T(8,128)}, f32[2,4096,128]{2,1,0:T(8,128)}, f32[2,128,128]{2,1,0:T(8,128)S(1)}, s32[]{:T(128)}, /*index=5*/s32[]{:T(128)}, s32[]{:T(128)}) while((s32[]{:T(128)}, f32[4096,512]{1,0:T(8,128)}, f32[2,4096,128]{2,1,0:T(8,128)}, f32[2,128,128]{2,1,0:T(8,128)S(1)}, s32[]{:T(128)}, ...), condition=%wide.region_3.3_spmd, body=%wide.region_1.2_spmd.sunk | while | flops 6545276928 | bytes 32047280 | solution.py:33
  2011.6 110.4 %while.45 = (s32[]{:T(128)}, f32[4096,512]{1,0:T(8,128)}, f32[2,4096,128]{2,1,0:T(8,128)}, f32[2,128,128]{2,1,0:T(8,128)S(1)}, s32[]{:T(128)}, /*index=5*/s32[]{:T(128)}, s32[]{:T(128)}) while((s32[]{:T(128)}, f32[4096,512]{1,0:T(8,128)}, f32[2,4096,128]{2,1,0:T(8,128)}, f32[2,128,128]{2,1,0:T(8,128)S(1)}, s32[]{:T(128)}, ...), condition=%wide.region_3.3_spmd, body=%wide.region_1.2_spmd.sunk | while | flops 6545276928 | bytes 32047280 | solution.py:33
  2136.5 110.4 %while.45 = (s32[]{:T(128)}, f32[4096,512]{1,0:T(8,128)}, f32[2,4096,128]{2,1,0:T(8,128)}, f32[2,128,128]{2,1,0:T(8,128)S(1)}, s32[]{:T(128)}, /*index=5*/s32[]{:T(128)}, s32[]{:T(128)}) while((s32[]{:T(128)}, f32[4096,512]{1,0:T(8,128)}, f32[2,4096,128]{2,1,0:T(8,128)}, f32[2,128,128]{2,1,0:T(8,128)S(1)}, s32[]{:T(128)}, ...), condition=%wide.region_3.3_spmd, body=%wide.region_1.2_spmd.sunk | while | flops 6545276928 | bytes 32047280 | solution.py:33
  2261.3 110.4 %while.45 = (s32[]{:T(128)}, f32[4096,512]{1,0:T(8,128)}, f32[2,4096,128]{2,1,0:T(8,128)}, f32[2,128,128]{2,1,0:T(8,128)S(1)}, s32[]{:T(128)}, /*index=5*/s32[]{:T(128)}, s32[]{:T(128)}) while((s32[]{:T(128)}, f32[4096,512]{1,0:T(8,128)}, f32[2,4096,128]{2,1,0:T(8,128)}, f32[2,128,128]{2,1,0:T(8,128)S(1)}, s32[]{:T(128)}, ...), condition=%wide.region_3.3_spmd, body=%wide.region_1.2_spmd.sunk | while | flops 6545276928 | bytes 32047280 | solution.py:33
  2386.2 110.4 %while.45 = (s32[]{:T(128)}, f32[4096,512]{1,0:T(8,128)}, f32[2,4096,128]{2,1,0:T(8,128)}, f32[2,128,128]{2,1,0:T(8,128)S(1)}, s32[]{:T(128)}, /*index=5*/s32[]{:T(128)}, s32[]{:T(128)}) while((s32[]{:T(128)}, f32[4096,512]{1,0:T(8,128)}, f32[2,4096,128]{2,1,0:T(8,128)}, f32[2,128,128]{2,1,0:T(8,128)S(1)}, s32[]{:T(128)}, ...), condition=%wide.region_3.3_spmd, body=%wide.region_1.2_spmd.sunk | while | flops 6545276928 | bytes 32047280 | solution.py:33
  2511.1 110.4 %while.45 = (s32[]{:T(128)}, f32[4096,512]{1,0:T(8,128)}, f32[2,4096,128]{2,1,0:T(8,128)}, f32[2,128,128]{2,1,0:T(8,128)S(1)}, s32[]{:T(128)}, /*index=5*/s32[]{:T(128)}, s32[]{:T(128)}) while((s32[]{:T(128)}, f32[4096,512]{1,0:T(8,128)}, f32[2,4096,128]{2,1,0:T(8,128)}, f32[2,128,128]{2,1,0:T(8,128)S(1)}, s32[]{:T(128)}, ...), condition=%wide.region_3.3_spmd, body=%wide.region_1.2_spmd.sunk | while | flops 6545276928 | bytes 32047280 | solution.py:33
  2635.9 110.4 %while.45 = (s32[]{:T(128)}, f32[4096,512]{1,0:T(8,128)}, f32[2,4096,128]{2,1,0:T(8,128)}, f32[2,128,128]{2,1,0:T(8,128)S(1)}, s32[]{:T(128)}, /*index=5*/s32[]{:T(128)}, s32[]{:T(128)}) while((s32[]{:T(128)}, f32[4096,512]{1,0:T(8,128)}, f32[2,4096,128]{2,1,0:T(8,128)}, f32[2,128,128]{2,1,0:T(8,128)S(1)}, s32[]{:T(128)}, ...), condition=%wide.region_3.3_spmd, body=%wide.region_1.2_spmd.sunk | while | flops 6545276928 | bytes 32047280 | solution.py:33
  2760.8 110.4 %while.45 = (s32[]{:T(128)}, f32[4096,512]{1,0:T(8,128)}, f32[2,4096,128]{2,1,0:T(8,128)}, f32[2,128,128]{2,1,0:T(8,128)S(1)}, s32[]{:T(128)}, /*index=5*/s32[]{:T(128)}, s32[]{:T(128)}) while((s32[]{:T(128)}, f32[4096,512]{1,0:T(8,128)}, f32[2,4096,128]{2,1,0:T(8,128)}, f32[2,128,128]{2,1,0:T(8,128)S(1)}, s32[]{:T(128)}, ...), condition=%wide.region_3.3_spmd, body=%wide.region_1.2_spmd.sunk | while | flops 6545276928 | bytes 32047280 | solution.py:33
  2885.6 110.4 %while.45 = (s32[]{:T(128)}, f32[4096,512]{1,0:T(8,128)}, f32[2,4096,128]{2,1,0:T(8,128)}, f32[2,128,128]{2,1,0:T(8,128)S(1)}, s32[]{:T(128)}, /*index=5*/s32[]{:T(128)}, s32[]{:T(128)}) while((s32[]{:T(128)}, f32[4096,512]{1,0:T(8,128)}, f32[2,4096,128]{2,1,0:T(8,128)}, f32[2,128,128]{2,1,0:T(8,128)S(1)}, s32[]{:T(128)}, ...), condition=%wide.region_3.3_spmd, body=%wide.region_1.2_spmd.sunk | while | flops 6545276928 | bytes 32047280 | solution.py:33
  3010.5 110.4 %while.45 = (s32[]{:T(128)}, f32[4096,512]{1,0:T(8,128)}, f32[2,4096,128]{2,1,0:T(8,128)}, f32[2,128,128]{2,1,0:T(8,128)S(1)}, s32[]{:T(128)}, /*index=5*/s32[]{:T(128)}, s32[]{:T(128)}) while((s32[]{:T(128)}, f32[4096,512]{1,0:T(8,128)}, f32[2,4096,128]{2,1,0:T(8,128)}, f32[2,128,128]{2,1,0:T(8,128)S(1)}, s32[]{:T(128)}, ...), condition=%wide.region_3.3_spmd, body=%wide.region_1.2_spmd.sunk | while | flops 6545276928 | bytes 32047280 | solution.py:33
  3135.4 110.4 %while.45 = (s32[]{:T(128)}, f32[4096,512]{1,0:T(8,128)}, f32[2,4096,128]{2,1,0:T(8,128)}, f32[2,128,128]{2,1,0:T(8,128)S(1)}, s32[]{:T(128)}, /*index=5*/s32[]{:T(128)}, s32[]{:T(128)}) while((s32[]{:T(128)}, f32[4096,512]{1,0:T(8,128)}, f32[2,4096,128]{2,1,0:T(8,128)}, f32[2,128,128]{2,1,0:T(8,128)S(1)}, s32[]{:T(128)}, ...), condition=%wide.region_3.3_spmd, body=%wide.region_1.2_spmd.sunk | while | flops 6545276928 | bytes 32047280 | solution.py:33
  3260.2 110.4 %while.45 = (s32[]{:T(128)}, f32[4096,512]{1,0:T(8,128)}, f32[2,4096,128]{2,1,0:T(8,128)}, f32[2,128,128]{2,1,0:T(8,128)S(1)}, s32[]{:T(128)}, /*index=5*/s32[]{:T(128)}, s32[]{:T(128)}) while((s32[]{:T(128)}, f32[4096,512]{1,0:T(8,128)}, f32[2,4096,128]{2,1,0:T(8,128)}, f32[2,128,128]{2,1,0:T(8,128)S(1)}, s32[]{:T(128)}, ...), condition=%wide.region_3.3_spmd, body=%wide.region_1.2_spmd.sunk | while | flops 6545276928 | bytes 32047280 | solution.py:33
  3385.1 110.4 %while.45 = (s32[]{:T(128)}, f32[4096,512]{1,0:T(8,128)}, f32[2,4096,128]{2,1,0:T(8,128)}, f32[2,128,128]{2,1,0:T(8,128)S(1)}, s32[]{:T(128)}, /*index=5*/s32[]{:T(128)}, s32[]{:T(128)}) while((s32[]{:T(128)}, f32[4096,512]{1,0:T(8,128)}, f32[2,4096,128]{2,1,0:T(8,128)}, f32[2,128,128]{2,1,0:T(8,128)S(1)}, s32[]{:T(128)}, ...), condition=%wide.region_3.3_spmd, body=%wide.region_1.2_spmd.sunk | while | flops 6545276928 | bytes 32047280 | solution.py:33
  3509.9 110.4 %while.45 = (s32[]{:T(128)}, f32[4096,512]{1,0:T(8,128)}, f32[2,4096,128]{2,1,0:T(8,128)}, f32[2,128,128]{2,1,0:T(8,128)S(1)}, s32[]{:T(128)}, /*index=5*/s32[]{:T(128)}, s32[]{:T(128)}) while((s32[]{:T(128)}, f32[4096,512]{1,0:T(8,128)}, f32[2,4096,128]{2,1,0:T(8,128)}, f32[2,128,128]{2,1,0:T(8,128)S(1)}, s32[]{:T(128)}, ...), condition=%wide.region_3.3_spmd, body=%wide.region_1.2_spmd.sunk | while | flops 6545276928 | bytes 32047280 | solution.py:33
  3634.8 110.4 %while.45 = (s32[]{:T(128)}, f32[4096,512]{1,0:T(8,128)}, f32[2,4096,128]{2,1,0:T(8,128)}, f32[2,128,128]{2,1,0:T(8,128)S(1)}, s32[]{:T(128)}, /*index=5*/s32[]{:T(128)}, s32[]{:T(128)}) while((s32[]{:T(128)}, f32[4096,512]{1,0:T(8,128)}, f32[2,4096,128]{2,1,0:T(8,128)}, f32[2,128,128]{2,1,0:T(8,128)S(1)}, s32[]{:T(128)}, ...), condition=%wide.region_3.3_spmd, body=%wide.region_1.2_spmd.sunk | while | flops 6545276928 | bytes 32047280 | solution.py:33
  3759.7 110.4 %while.45 = (s32[]{:T(128)}, f32[4096,512]{1,0:T(8,128)}, f32[2,4096,128]{2,1,0:T(8,128)}, f32[2,128,128]{2,1,0:T(8,128)S(1)}, s32[]{:T(128)}, /*index=5*/s32[]{:T(128)}, s32[]{:T(128)}) while((s32[]{:T(128)}, f32[4096,512]{1,0:T(8,128)}, f32[2,4096,128]{2,1,0:T(8,128)}, f32[2,128,128]{2,1,0:T(8,128)S(1)}, s32[]{:T(128)}, ...), condition=%wide.region_3.3_spmd, body=%wide.region_1.2_spmd.sunk | while | flops 6545276928 | bytes 32047280 | solution.py:33
  3884.5 110.4 %while.45 = (s32[]{:T(128)}, f32[4096,512]{1,0:T(8,128)}, f32[2,4096,128]{2,1,0:T(8,128)}, f32[2,128,128]{2,1,0:T(8,128)S(1)}, s32[]{:T(128)}, /*index=5*/s32[]{:T(128)}, s32[]{:T(128)}) while((s32[]{:T(128)}, f32[4096,512]{1,0:T(8,128)}, f32[2,4096,128]{2,1,0:T(8,128)}, f32[2,128,128]{2,1,0:T(8,128)S(1)}, s32[]{:T(128)}, ...), condition=%wide.region_3.3_spmd, body=%wide.region_1.2_spmd.sunk | while | flops 6545276928 | bytes 32047280 | solution.py:33
  4009.4 110.4 %while.45 = (s32[]{:T(128)}, f32[4096,512]{1,0:T(8,128)}, f32[2,4096,128]{2,1,0:T(8,128)}, f32[2,128,128]{2,1,0:T(8,128)S(1)}, s32[]{:T(128)}, /*index=5*/s32[]{:T(128)}, s32[]{:T(128)}) while((s32[]{:T(128)}, f32[4096,512]{1,0:T(8,128)}, f32[2,4096,128]{2,1,0:T(8,128)}, f32[2,128,128]{2,1,0:T(8,128)S(1)}, s32[]{:T(128)}, ...), condition=%wide.region_3.3_spmd, body=%wide.region_1.2_spmd.sunk | while | flops 6545276928 | bytes 32047280 | solution.py:33
  4134.2 110.4 %while.45 = (s32[]{:T(128)}, f32[4096,512]{1,0:T(8,128)}, f32[2,4096,128]{2,1,0:T(8,128)}, f32[2,128,128]{2,1,0:T(8,128)S(1)}, s32[]{:T(128)}, /*index=5*/s32[]{:T(128)}, s32[]{:T(128)}) while((s32[]{:T(128)}, f32[4096,512]{1,0:T(8,128)}, f32[2,4096,128]{2,1,0:T(8,128)}, f32[2,128,128]{2,1,0:T(8,128)S(1)}, s32[]{:T(128)}, ...), condition=%wide.region_3.3_spmd, body=%wide.region_1.2_spmd.sunk | while | flops 6545276928 | bytes 32047280 | solution.py:33
  4259.1 110.4 %while.45 = (s32[]{:T(128)}, f32[4096,512]{1,0:T(8,128)}, f32[2,4096,128]{2,1,0:T(8,128)}, f32[2,128,128]{2,1,0:T(8,128)S(1)}, s32[]{:T(128)}, /*index=5*/s32[]{:T(128)}, s32[]{:T(128)}) while((s32[]{:T(128)}, f32[4096,512]{1,0:T(8,128)}, f32[2,4096,128]{2,1,0:T(8,128)}, f32[2,128,128]{2,1,0:T(8,128)S(1)}, s32[]{:T(128)}, ...), condition=%wide.region_3.3_spmd, body=%wide.region_1.2_spmd.sunk | while | flops 6545276928 | bytes 32047280 | solution.py:33
  4383.9 110.4 %while.45 = (s32[]{:T(128)}, f32[4096,512]{1,0:T(8,128)}, f32[2,4096,128]{2,1,0:T(8,128)}, f32[2,128,128]{2,1,0:T(8,128)S(1)}, s32[]{:T(128)}, /*index=5*/s32[]{:T(128)}, s32[]{:T(128)}) while((s32[]{:T(128)}, f32[4096,512]{1,0:T(8,128)}, f32[2,4096,128]{2,1,0:T(8,128)}, f32[2,128,128]{2,1,0:T(8,128)S(1)}, s32[]{:T(128)}, ...), condition=%wide.region_3.3_spmd, body=%wide.region_1.2_spmd.sunk | while | flops 6545276928 | bytes 32047280 | solution.py:33
  4508.8 110.4 %while.45 = (s32[]{:T(128)}, f32[4096,512]{1,0:T(8,128)}, f32[2,4096,128]{2,1,0:T(8,128)}, f32[2,128,128]{2,1,0:T(8,128)S(1)}, s32[]{:T(128)}, /*index=5*/s32[]{:T(128)}, s32[]{:T(128)}) while((s32[]{:T(128)}, f32[4096,512]{1,0:T(8,128)}, f32[2,4096,128]{2,1,0:T(8,128)}, f32[2,128,128]{2,1,0:T(8,128)S(1)}, s32[]{:T(128)}, ...), condition=%wide.region_3.3_spmd, body=%wide.region_1.2_spmd.sunk | while | flops 6545276928 | bytes 32047280 | solution.py:33
  4633.7 110.4 %while.45 = (s32[]{:T(128)}, f32[4096,512]{1,0:T(8,128)}, f32[2,4096,128]{2,1,0:T(8,128)}, f32[2,128,128]{2,1,0:T(8,128)S(1)}, s32[]{:T(128)}, /*index=5*/s32[]{:T(128)}, s32[]{:T(128)}) while((s32[]{:T(128)}, f32[4096,512]{1,0:T(8,128)}, f32[2,4096,128]{2,1,0:T(8,128)}, f32[2,128,128]{2,1,0:T(8,128)S(1)}, s32[]{:T(128)}, ...), condition=%wide.region_3.3_spmd, body=%wide.region_1.2_spmd.sunk | while | flops 6545276928 | bytes 32047280 | solution.py:33
  4758.5 110.4 %while.45 = (s32[]{:T(128)}, f32[4096,512]{1,0:T(8,128)}, f32[2,4096,128]{2,1,0:T(8,128)}, f32[2,128,128]{2,1,0:T(8,128)S(1)}, s32[]{:T(128)}, /*index=5*/s32[]{:T(128)}, s32[]{:T(128)}) while((s32[]{:T(128)}, f32[4096,512]{1,0:T(8,128)}, f32[2,4096,128]{2,1,0:T(8,128)}, f32[2,128,128]{2,1,0:T(8,128)S(1)}, s32[]{:T(128)}, ...), condition=%wide.region_3.3_spmd, body=%wide.region_1.2_spmd.sunk | while | flops 6545276928 | bytes 32047280 | solution.py:33
  4883.4 110.4 %while.45 = (s32[]{:T(128)}, f32[4096,512]{1,0:T(8,128)}, f32[2,4096,128]{2,1,0:T(8,128)}, f32[2,128,128]{2,1,0:T(8,128)S(1)}, s32[]{:T(128)}, /*index=5*/s32[]{:T(128)}, s32[]{:T(128)}) while((s32[]{:T(128)}, f32[4096,512]{1,0:T(8,128)}, f32[2,4096,128]{2,1,0:T(8,128)}, f32[2,128,128]{2,1,0:T(8,128)S(1)}, s32[]{:T(128)}, ...), condition=%wide.region_3.3_spmd, body=%wide.region_1.2_spmd.sunk | while | flops 6545276928 | bytes 32047280 | solution.py:33
  5008.2 110.4 %while.45 = (s32[]{:T(128)}, f32[4096,512]{1,0:T(8,128)}, f32[2,4096,128]{2,1,0:T(8,128)}, f32[2,128,128]{2,1,0:T(8,128)S(1)}, s32[]{:T(128)}, /*index=5*/s32[]{:T(128)}, s32[]{:T(128)}) while((s32[]{:T(128)}, f32[4096,512]{1,0:T(8,128)}, f32[2,4096,128]{2,1,0:T(8,128)}, f32[2,128,128]{2,1,0:T(8,128)S(1)}, s32[]{:T(128)}, ...), condition=%wide.region_3.3_spmd, body=%wide.region_1.2_spmd.sunk | while | flops 6545276928 | bytes 32047280 | solution.py:33
  5133.1 110.4 %while.45 = (s32[]{:T(128)}, f32[4096,512]{1,0:T(8,128)}, f32[2,4096,128]{2,1,0:T(8,128)}, f32[2,128,128]{2,1,0:T(8,128)S(1)}, s32[]{:T(128)}, /*index=5*/s32[]{:T(128)}, s32[]{:T(128)}) while((s32[]{:T(128)}, f32[4096,512]{1,0:T(8,128)}, f32[2,4096,128]{2,1,0:T(8,128)}, f32[2,128,128]{2,1,0:T(8,128)S(1)}, s32[]{:T(128)}, ...), condition=%wide.region_3.3_spmd, body=%wide.region_1.2_spmd.sunk | while | flops 6545276928 | bytes 32047280 | solution.py:33
  5258.0 110.4 %while.45 = (s32[]{:T(128)}, f32[4096,512]{1,0:T(8,128)}, f32[2,4096,128]{2,1,0:T(8,128)}, f32[2,128,128]{2,1,0:T(8,128)S(1)}, s32[]{:T(128)}, /*index=5*/s32[]{:T(128)}, s32[]{:T(128)}) while((s32[]{:T(128)}, f32[4096,512]{1,0:T(8,128)}, f32[2,4096,128]{2,1,0:T(8,128)}, f32[2,128,128]{2,1,0:T(8,128)S(1)}, s32[]{:T(128)}, ...), condition=%wide.region_3.3_spmd, body=%wide.region_1.2_spmd.sunk | while | flops 6545276928 | bytes 32047280 | solution.py:33
  5382.8 110.4 %while.45 = (s32[]{:T(128)}, f32[4096,512]{1,0:T(8,128)}, f32[2,4096,128]{2,1,0:T(8,128)}, f32[2,128,128]{2,1,0:T(8,128)S(1)}, s32[]{:T(128)}, /*index=5*/s32[]{:T(128)}, s32[]{:T(128)}) while((s32[]{:T(128)}, f32[4096,512]{1,0:T(8,128)}, f32[2,4096,128]{2,1,0:T(8,128)}, f32[2,128,128]{2,1,0:T(8,128)S(1)}, s32[]{:T(128)}, ...), condition=%wide.region_3.3_spmd, body=%wide.region_1.2_spmd.sunk | while | flops 6545276928 | bytes 32047280 | solution.py:33
  5507.7 110.4 %while.45 = (s32[]{:T(128)}, f32[4096,512]{1,0:T(8,128)}, f32[2,4096,128]{2,1,0:T(8,128)}, f32[2,128,128]{2,1,0:T(8,128)S(1)}, s32[]{:T(128)}, /*index=5*/s32[]{:T(128)}, s32[]{:T(128)}) while((s32[]{:T(128)}, f32[4096,512]{1,0:T(8,128)}, f32[2,4096,128]{2,1,0:T(8,128)}, f32[2,128,128]{2,1,0:T(8,128)S(1)}, s32[]{:T(128)}, ...), condition=%wide.region_3.3_spmd, body=%wide.region_1.2_spmd.sunk | while | flops 6545276928 | bytes 32047280 | solution.py:33
  5632.5 110.4 %while.45 = (s32[]{:T(128)}, f32[4096,512]{1,0:T(8,128)}, f32[2,4096,128]{2,1,0:T(8,128)}, f32[2,128,128]{2,1,0:T(8,128)S(1)}, s32[]{:T(128)}, /*index=5*/s32[]{:T(128)}, s32[]{:T(128)}) while((s32[]{:T(128)}, f32[4096,512]{1,0:T(8,128)}, f32[2,4096,128]{2,1,0:T(8,128)}, f32[2,128,128]{2,1,0:T(8,128)S(1)}, s32[]{:T(128)}, ...), condition=%wide.region_3.3_spmd, body=%wide.region_1.2_spmd.sunk | while | flops 6545276928 | bytes 32047280 | solution.py:33
  5757.4 110.4 %while.45 = (s32[]{:T(128)}, f32[4096,512]{1,0:T(8,128)}, f32[2,4096,128]{2,1,0:T(8,128)}, f32[2,128,128]{2,1,0:T(8,128)S(1)}, s32[]{:T(128)}, /*index=5*/s32[]{:T(128)}, s32[]{:T(128)}) while((s32[]{:T(128)}, f32[4096,512]{1,0:T(8,128)}, f32[2,4096,128]{2,1,0:T(8,128)}, f32[2,128,128]{2,1,0:T(8,128)S(1)}, s32[]{:T(128)}, ...), condition=%wide.region_3.3_spmd, body=%wide.region_1.2_spmd.sunk | while | flops 6545276928 | bytes 32047280 | solution.py:33
  5882.3 110.4 %while.45 = (s32[]{:T(128)}, f32[4096,512]{1,0:T(8,128)}, f32[2,4096,128]{2,1,0:T(8,128)}, f32[2,128,128]{2,1,0:T(8,128)S(1)}, s32[]{:T(128)}, /*index=5*/s32[]{:T(128)}, s32[]{:T(128)}) while((s32[]{:T(128)}, f32[4096,512]{1,0:T(8,128)}, f32[2,4096,128]{2,1,0:T(8,128)}, f32[2,128,128]{2,1,0:T(8,128)S(1)}, s32[]{:T(128)}, ...), condition=%wide.region_3.3_spmd, body=%wide.region_1.2_spmd.sunk | while | flops 6545276928 | bytes 32047280 | solution.py:33
  6007.1 110.4 %while.45 = (s32[]{:T(128)}, f32[4096,512]{1,0:T(8,128)}, f32[2,4096,128]{2,1,0:T(8,128)}, f32[2,128,128]{2,1,0:T(8,128)S(1)}, s32[]{:T(128)}, /*index=5*/s32[]{:T(128)}, s32[]{:T(128)}) while((s32[]{:T(128)}, f32[4096,512]{1,0:T(8,128)}, f32[2,4096,128]{2,1,0:T(8,128)}, f32[2,128,128]{2,1,0:T(8,128)S(1)}, s32[]{:T(128)}, ...), condition=%wide.region_3.3_spmd, body=%wide.region_1.2_spmd.sunk | while | flops 6545276928 | bytes 32047280 | solution.py:33
  6132.0 110.4 %while.45 = (s32[]{:T(128)}, f32[4096,512]{1,0:T(8,128)}, f32[2,4096,128]{2,1,0:T(8,128)}, f32[2,128,128]{2,1,0:T(8,128)S(1)}, s32[]{:T(128)}, /*index=5*/s32[]{:T(128)}, s32[]{:T(128)}) while((s32[]{:T(128)}, f32[4096,512]{1,0:T(8,128)}, f32[2,4096,128]{2,1,0:T(8,128)}, f32[2,128,128]{2,1,0:T(8,128)S(1)}, s32[]{:T(128)}, ...), condition=%wide.region_3.3_spmd, body=%wide.region_1.2_spmd.sunk | while | flops 6545276928 | bytes 32047280 | solution.py:33
  6256.8 110.4 %while.45 = (s32[]{:T(128)}, f32[4096,512]{1,0:T(8,128)}, f32[2,4096,128]{2,1,0:T(8,128)}, f32[2,128,128]{2,1,0:T(8,128)S(1)}, s32[]{:T(128)}, /*index=5*/s32[]{:T(128)}, s32[]{:T(128)}) while((s32[]{:T(128)}, f32[4096,512]{1,0:T(8,128)}, f32[2,4096,128]{2,1,0:T(8,128)}, f32[2,128,128]{2,1,0:T(8,128)S(1)}, s32[]{:T(128)}, ...), condition=%wide.region_3.3_spmd, body=%wide.region_1.2_spmd.sunk | while | flops 6545276928 | bytes 32047280 | solution.py:33
  6381.7 110.4 %while.45 = (s32[]{:T(128)}, f32[4096,512]{1,0:T(8,128)}, f32[2,4096,128]{2,1,0:T(8,128)}, f32[2,128,128]{2,1,0:T(8,128)S(1)}, s32[]{:T(128)}, /*index=5*/s32[]{:T(128)}, s32[]{:T(128)}) while((s32[]{:T(128)}, f32[4096,512]{1,0:T(8,128)}, f32[2,4096,128]{2,1,0:T(8,128)}, f32[2,128,128]{2,1,0:T(8,128)S(1)}, s32[]{:T(128)}, ...), condition=%wide.region_3.3_spmd, body=%wide.region_1.2_spmd.sunk | while | flops 6545276928 | bytes 32047280 | solution.py:33
  6506.5 110.4 %while.45 = (s32[]{:T(128)}, f32[4096,512]{1,0:T(8,128)}, f32[2,4096,128]{2,1,0:T(8,128)}, f32[2,128,128]{2,1,0:T(8,128)S(1)}, s32[]{:T(128)}, /*index=5*/s32[]{:T(128)}, s32[]{:T(128)}) while((s32[]{:T(128)}, f32[4096,512]{1,0:T(8,128)}, f32[2,4096,128]{2,1,0:T(8,128)}, f32[2,128,128]{2,1,0:T(8,128)S(1)}, s32[]{:T(128)}, ...), condition=%wide.region_3.3_spmd, body=%wide.region_1.2_spmd.sunk | while | flops 6545276928 | bytes 32047280 | solution.py:33
  6631.4 110.4 %while.45 = (s32[]{:T(128)}, f32[4096,512]{1,0:T(8,128)}, f32[2,4096,128]{2,1,0:T(8,128)}, f32[2,128,128]{2,1,0:T(8,128)S(1)}, s32[]{:T(128)}, /*index=5*/s32[]{:T(128)}, s32[]{:T(128)}) while((s32[]{:T(128)}, f32[4096,512]{1,0:T(8,128)}, f32[2,4096,128]{2,1,0:T(8,128)}, f32[2,128,128]{2,1,0:T(8,128)S(1)}, s32[]{:T(128)}, ...), condition=%wide.region_3.3_spmd, body=%wide.region_1.2_spmd.sunk | while | flops 6545276928 | bytes 32047280 | solution.py:33
  6756.3 110.4 %while.45 = (s32[]{:T(128)}, f32[4096,512]{1,0:T(8,128)}, f32[2,4096,128]{2,1,0:T(8,128)}, f32[2,128,128]{2,1,0:T(8,128)S(1)}, s32[]{:T(128)}, /*index=5*/s32[]{:T(128)}, s32[]{:T(128)}) while((s32[]{:T(128)}, f32[4096,512]{1,0:T(8,128)}, f32[2,4096,128]{2,1,0:T(8,128)}, f32[2,128,128]{2,1,0:T(8,128)S(1)}, s32[]{:T(128)}, ...), condition=%wide.region_3.3_spmd, body=%wide.region_1.2_spmd.sunk | while | flops 6545276928 | bytes 32047280 | solution.py:33
  6881.1 110.4 %while.45 = (s32[]{:T(128)}, f32[4096,512]{1,0:T(8,128)}, f32[2,4096,128]{2,1,0:T(8,128)}, f32[2,128,128]{2,1,0:T(8,128)S(1)}, s32[]{:T(128)}, /*index=5*/s32[]{:T(128)}, s32[]{:T(128)}) while((s32[]{:T(128)}, f32[4096,512]{1,0:T(8,128)}, f32[2,4096,128]{2,1,0:T(8,128)}, f32[2,128,128]{2,1,0:T(8,128)S(1)}, s32[]{:T(128)}, ...), condition=%wide.region_3.3_spmd, body=%wide.region_1.2_spmd.sunk | while | flops 6545276928 | bytes 32047280 | solution.py:33
  7006.0 110.4 %while.45 = (s32[]{:T(128)}, f32[4096,512]{1,0:T(8,128)}, f32[2,4096,128]{2,1,0:T(8,128)}, f32[2,128,128]{2,1,0:T(8,128)S(1)}, s32[]{:T(128)}, /*index=5*/s32[]{:T(128)}, s32[]{:T(128)}) while((s32[]{:T(128)}, f32[4096,512]{1,0:T(8,128)}, f32[2,4096,128]{2,1,0:T(8,128)}, f32[2,128,128]{2,1,0:T(8,128)S(1)}, s32[]{:T(128)}, ...), condition=%wide.region_3.3_spmd, body=%wide.region_1.2_spmd.sunk | while | flops 6545276928 | bytes 32047280 | solution.py:33
  7130.8 110.4 %while.45 = (s32[]{:T(128)}, f32[4096,512]{1,0:T(8,128)}, f32[2,4096,128]{2,1,0:T(8,128)}, f32[2,128,128]{2,1,0:T(8,128)S(1)}, s32[]{:T(128)}, /*index=5*/s32[]{:T(128)}, s32[]{:T(128)}) while((s32[]{:T(128)}, f32[4096,512]{1,0:T(8,128)}, f32[2,4096,128]{2,1,0:T(8,128)}, f32[2,128,128]{2,1,0:T(8,128)S(1)}, s32[]{:T(128)}, ...), condition=%wide.region_3.3_spmd, body=%wide.region_1.2_spmd.sunk | while | flops 6545276928 | bytes 32047280 | solution.py:33
  7255.7 110.4 %while.45 = (s32[]{:T(128)}, f32[4096,512]{1,0:T(8,128)}, f32[2,4096,128]{2,1,0:T(8,128)}, f32[2,128,128]{2,1,0:T(8,128)S(1)}, s32[]{:T(128)}, /*index=5*/s32[]{:T(128)}, s32[]{:T(128)}) while((s32[]{:T(128)}, f32[4096,512]{1,0:T(8,128)}, f32[2,4096,128]{2,1,0:T(8,128)}, f32[2,128,128]{2,1,0:T(8,128)S(1)}, s32[]{:T(128)}, ...), condition=%wide.region_3.3_spmd, body=%wide.region_1.2_spmd.sunk | while | flops 6545276928 | bytes 32047280 | solution.py:33
  7380.6 110.4 %while.45 = (s32[]{:T(128)}, f32[4096,512]{1,0:T(8,128)}, f32[2,4096,128]{2,1,0:T(8,128)}, f32[2,128,128]{2,1,0:T(8,128)S(1)}, s32[]{:T(128)}, /*index=5*/s32[]{:T(128)}, s32[]{:T(128)}) while((s32[]{:T(128)}, f32[4096,512]{1,0:T(8,128)}, f32[2,4096,128]{2,1,0:T(8,128)}, f32[2,128,128]{2,1,0:T(8,128)S(1)}, s32[]{:T(128)}, ...), condition=%wide.region_3.3_spmd, body=%wide.region_1.2_spmd.sunk | while | flops 6545276928 | bytes 32047280 | solution.py:33
  7505.4 110.4 %while.45 = (s32[]{:T(128)}, f32[4096,512]{1,0:T(8,128)}, f32[2,4096,128]{2,1,0:T(8,128)}, f32[2,128,128]{2,1,0:T(8,128)S(1)}, s32[]{:T(128)}, /*index=5*/s32[]{:T(128)}, s32[]{:T(128)}) while((s32[]{:T(128)}, f32[4096,512]{1,0:T(8,128)}, f32[2,4096,128]{2,1,0:T(8,128)}, f32[2,128,128]{2,1,0:T(8,128)S(1)}, s32[]{:T(128)}, ...), condition=%wide.region_3.3_spmd, body=%wide.region_1.2_spmd.sunk | while | flops 6545276928 | bytes 32047280 | solution.py:33
  7630.3 110.4 %while.45 = (s32[]{:T(128)}, f32[4096,512]{1,0:T(8,128)}, f32[2,4096,128]{2,1,0:T(8,128)}, f32[2,128,128]{2,1,0:T(8,128)S(1)}, s32[]{:T(128)}, /*index=5*/s32[]{:T(128)}, s32[]{:T(128)}) while((s32[]{:T(128)}, f32[4096,512]{1,0:T(8,128)}, f32[2,4096,128]{2,1,0:T(8,128)}, f32[2,128,128]{2,1,0:T(8,128)S(1)}, s32[]{:T(128)}, ...), condition=%wide.region_3.3_spmd, body=%wide.region_1.2_spmd.sunk | while | flops 6545276928 | bytes 32047280 | solution.py:33
  7755.1 110.4 %while.45 = (s32[]{:T(128)}, f32[4096,512]{1,0:T(8,128)}, f32[2,4096,128]{2,1,0:T(8,128)}, f32[2,128,128]{2,1,0:T(8,128)S(1)}, s32[]{:T(128)}, /*index=5*/s32[]{:T(128)}, s32[]{:T(128)}) while((s32[]{:T(128)}, f32[4096,512]{1,0:T(8,128)}, f32[2,4096,128]{2,1,0:T(8,128)}, f32[2,128,128]{2,1,0:T(8,128)S(1)}, s32[]{:T(128)}, ...), condition=%wide.region_3.3_spmd, body=%wide.region_1.2_spmd.sunk | while | flops 6545276928 | bytes 32047280 | solution.py:33
  7880.0 110.4 %while.45 = (s32[]{:T(128)}, f32[4096,512]{1,0:T(8,128)}, f32[2,4096,128]{2,1,0:T(8,128)}, f32[2,128,128]{2,1,0:T(8,128)S(1)}, s32[]{:T(128)}, /*index=5*/s32[]{:T(128)}, s32[]{:T(128)}) while((s32[]{:T(128)}, f32[4096,512]{1,0:T(8,128)}, f32[2,4096,128]{2,1,0:T(8,128)}, f32[2,128,128]{2,1,0:T(8,128)S(1)}, s32[]{:T(128)}, ...), condition=%wide.region_3.3_spmd, body=%wide.region_1.2_spmd.sunk | while | flops 6545276928 | bytes 32047280 | solution.py:33
  8004.9 110.4 %while.45 = (s32[]{:T(128)}, f32[4096,512]{1,0:T(8,128)}, f32[2,4096,128]{2,1,0:T(8,128)}, f32[2,128,128]{2,1,0:T(8,128)S(1)}, s32[]{:T(128)}, /*index=5*/s32[]{:T(128)}, s32[]{:T(128)}) while((s32[]{:T(128)}, f32[4096,512]{1,0:T(8,128)}, f32[2,4096,128]{2,1,0:T(8,128)}, f32[2,128,128]{2,1,0:T(8,128)S(1)}, s32[]{:T(128)}, ...), condition=%wide.region_3.3_spmd, body=%wide.region_1.2_spmd.sunk | while | flops 6545276928 | bytes 32047280 | solution.py:33
  (1157 shorter events, 8215.4 us)
Async XLA Ops:
  6.5 99.7 %all-to-all-start = ((f32[4,4096,128]{2,1,0:T(8,128)}), f32[4,4096,128]{2,1,0:T(8,128)}, u32[]{:S(2)}, u32[]{:S(2)}) async-start(f32[4,4096,128]{2,1,0:T(8,128)} %bitcast.32), calls=%async_computation | async-start | bytes 16777216 | tf_op jit(solution)/shard_map/all_to_all | solution.py:15
  263.6 42.7 all-reduce.2.cloned.1.call-start
  388.5 42.7 all-reduce.2.cloned.1.call-start
  513.3 42.7 all-reduce.2.cloned.1.call-start
  638.2 42.7 all-reduce.2.cloned.1.call-start
  763.0 42.7 all-reduce.2.cloned.1.call-start
  887.9 42.7 all-reduce.2.cloned.1.call-start
  1012.8 42.7 all-reduce.2.cloned.1.call-start
  1137.6 42.7 all-reduce.2.cloned.1.call-start
  1262.5 42.7 all-reduce.2.cloned.1.call-start
  1387.3 42.7 all-reduce.2.cloned.1.call-start
  1512.2 42.7 all-reduce.2.cloned.1.call-start
  1637.0 42.7 all-reduce.2.cloned.1.call-start
  1761.9 42.7 all-reduce.2.cloned.1.call-start
  1886.8 42.7 all-reduce.2.cloned.1.call-start
  2011.6 42.7 all-reduce.2.cloned.1.call-start
  2136.5 42.7 all-reduce.2.cloned.1.call-start
  2261.3 42.7 all-reduce.2.cloned.1.call-start
  2386.2 42.7 all-reduce.2.cloned.1.call-start
  2511.1 42.7 all-reduce.2.cloned.1.call-start
  2635.9 42.7 all-reduce.2.cloned.1.call-start
  2760.8 42.7 all-reduce.2.cloned.1.call-start
  2885.6 42.7 all-reduce.2.cloned.1.call-start
  3010.5 42.7 all-reduce.2.cloned.1.call-start
  3135.4 42.7 all-reduce.2.cloned.1.call-start
  3260.2 42.7 all-reduce.2.cloned.1.call-start
  3385.1 42.7 all-reduce.2.cloned.1.call-start
  3509.9 42.7 all-reduce.2.cloned.1.call-start
  3634.8 42.7 all-reduce.2.cloned.1.call-start
  3759.7 42.7 all-reduce.2.cloned.1.call-start
  3884.5 42.7 all-reduce.2.cloned.1.call-start
  4009.4 42.7 all-reduce.2.cloned.1.call-start
  4134.2 42.7 all-reduce.2.cloned.1.call-start
  4259.1 42.7 all-reduce.2.cloned.1.call-start
  4383.9 42.7 all-reduce.2.cloned.1.call-start
  4508.8 42.7 all-reduce.2.cloned.1.call-start
  4633.7 42.7 all-reduce.2.cloned.1.call-start
  4758.5 42.7 all-reduce.2.cloned.1.call-start
  4883.4 42.7 all-reduce.2.cloned.1.call-start
  5008.2 42.7 all-reduce.2.cloned.1.call-start
  5133.1 42.7 all-reduce.2.cloned.1.call-start
  5258.0 42.7 all-reduce.2.cloned.1.call-start
  5382.8 42.7 all-reduce.2.cloned.1.call-start
  5507.7 42.7 all-reduce.2.cloned.1.call-start
  5632.5 42.7 all-reduce.2.cloned.1.call-start
  5757.4 42.7 all-reduce.2.cloned.1.call-start
  5882.3 42.7 all-reduce.2.cloned.1.call-start
  6007.1 42.7 all-reduce.2.cloned.1.call-start
  6132.0 42.7 all-reduce.2.cloned.1.call-start
  6256.8 42.7 all-reduce.2.cloned.1.call-start
  6381.7 42.7 all-reduce.2.cloned.1.call-start
  6506.5 42.7 all-reduce.2.cloned.1.call-start
  6631.4 42.7 all-reduce.2.cloned.1.call-start
  6756.3 42.7 all-reduce.2.cloned.1.call-start
  6881.1 42.7 all-reduce.2.cloned.1.call-start
  7006.0 42.7 all-reduce.2.cloned.1.call-start
  7130.8 42.7 all-reduce.2.cloned.1.call-start
  7255.7 42.7 all-reduce.2.cloned.1.call-start
  7380.6 42.7 all-reduce.2.cloned.1.call-start
  7505.4 42.7 all-reduce.2.cloned.1.call-start
  7630.3 42.7 all-reduce.2.cloned.1.call-start
  7755.1 42.7 all-reduce.2.cloned.1.call-start
  7880.0 42.7 all-reduce.2.cloned.1.call-start
  8004.9 42.7 all-reduce.2.cloned.1.call-start
  (129 other events, 3625.1 us)
Sparse Core Ops, SparseCore 0:
  148.7 32.7 all-reduce.1
  273.5 32.7 all-reduce.1
  398.4 32.7 all-reduce.1
  523.3 32.7 all-reduce.1
  648.1 32.7 all-reduce.1
  773.0 32.7 all-reduce.1
  897.8 32.7 all-reduce.1
  1022.7 32.7 all-reduce.1
  1147.5 32.7 all-reduce.1
  1272.4 32.7 all-reduce.1
  1397.3 32.7 all-reduce.1
  1522.1 32.7 all-reduce.1
  1647.0 32.7 all-reduce.1
  1771.8 32.7 all-reduce.1
  1896.7 32.7 all-reduce.1
  2021.6 32.7 all-reduce.1
  2146.4 32.7 all-reduce.1
  2271.3 32.7 all-reduce.1
  2396.1 32.7 all-reduce.1
  2521.0 32.7 all-reduce.1
  2645.9 32.7 all-reduce.1
  2770.7 32.7 all-reduce.1
  2895.6 32.7 all-reduce.1
  3020.4 32.7 all-reduce.1
  3145.3 32.7 all-reduce.1
  3270.2 32.7 all-reduce.1
  3395.0 32.7 all-reduce.1
  3519.9 32.7 all-reduce.1
  3644.7 32.7 all-reduce.1
  3769.6 32.7 all-reduce.1
  3894.4 32.7 all-reduce.1
  4019.3 32.7 all-reduce.1
  4144.2 32.7 all-reduce.1
  4269.0 32.7 all-reduce.1
  4393.9 32.7 all-reduce.1
  4518.7 32.7 all-reduce.1
  4643.6 32.7 all-reduce.1
  4768.5 32.7 all-reduce.1
  4893.3 32.7 all-reduce.1
  5018.2 32.7 all-reduce.1
  5143.0 32.7 all-reduce.1
  5267.9 32.7 all-reduce.1
  5392.8 32.7 all-reduce.1
  5517.6 32.7 all-reduce.1
  5642.5 32.7 all-reduce.1
  5767.3 32.7 all-reduce.1
  5892.2 32.7 all-reduce.1
  6017.0 32.7 all-reduce.1
  6141.9 32.7 all-reduce.1
  6266.8 32.7 all-reduce.1
  6391.6 32.7 all-reduce.1
  6516.5 32.7 all-reduce.1
  6641.3 32.7 all-reduce.1
  6766.2 32.7 all-reduce.1
  6891.1 32.7 all-reduce.1
  7015.9 32.7 all-reduce.1
  7140.8 32.7 all-reduce.1
  7265.6 32.7 all-reduce.1
  7390.5 32.7 all-reduce.1
  7515.4 32.7 all-reduce.1
  7640.2 32.7 all-reduce.1
  7765.1 32.7 all-reduce.1
  7889.9 32.7 all-reduce.1
  8014.8 32.7 all-reduce.1
  (128 shorter events, 2729.5 us)
where the time goes:
time: 8130 us; the launch traced here: 8120 us
  waiting for transfers between devices  4780 us (59%)
  matrix products  2930 us (36%)
  local copies, waits for them, and re-layouts  268 us (3%)
  blocking collectives  121 us (1%)
    psum x128, waiting for transfers between devices, panel_step(): w_full = lax.psum(w_part, 'row')  4130 us
    dot_general x128, matrix products, panel_step(): jnp.dot(v_j, y_mat, precision=HIGHEST, preferred_element_type=jnp.float32)  1510 us
    dot_general x128, matrix products, panel_step(): jnp.einsum('na,nk->ak', v_j, x_in, precision=HIGHEST, preferred_element_t...  1250 us
    all_gather x64, waiting for transfers between devices, group_step(): v_group = lax.all_gather(v_blk, 'col', axis=0)  552 us
    dynamic_slice x64, local copies, waits for them, and re-layouts, group_step(): lax.dynamic_slice_in_dim(v_loc, group_idx * panel_width, panel_width, axi...  195 us
    dot_general x128, matrix products, panel_step(): jnp.dot(t_j, w_full, precision=HIGHEST, preferred_element_type=jnp.float32)  168 us
  transfers between devices with their start and end apart: 193, of which 193 were waited for; matrix products, arithmetic and copies ran while one was open for 1% of the time, Pallas kernels for 0%

commit v1 on v0

v1 whole, which is shorter than its diff:
```python
import functools

import jax
import jax.numpy as jnp
from jax import lax
from jax.experimental import pallas as pl
from jax.experimental.pallas import tpu as pltpu
from jax.sharding import PartitionSpec as P

HIGHEST = lax.Precision.HIGHEST
F32 = jnp.float32
BF16 = jnp.bfloat16
MESH = pl.DeviceIdType.MESH
NN = (((1,), (0,)), ((), ()))
NT = (((1,), (1,)), ((), ()))
C = 128
B = 256
SH = 32


def dg(a, b, dims):
    return lax.dot_general(a, b, dims, preferred_element_type=F32)


def split3(x):
    x0 = x.astype(BF16)
    r1 = x - x0.astype(F32)
    x1 = r1.astype(BF16)
    x2 = (r1 - x1.astype(F32)).astype(BF16)
    return x0, x1, x2


def kernel(R, NB, t_hbm, v_hbm, z_hbm, out_hbm,
           xT, vst, vb, tb, ysp, xs, wacc, wsend, wrecv, ysend, yT,
           z_send, z_recv, z_loc, v_send, v_recv, v_loc, t_sem,
           rs_send, rs_recv, ag_send, ag_recv, o_sem, vfree):
    NL = xT.shape[1]
    NT_TILES = NL // R
    TB = R // 64
    me = lax.axis_index('row')
    e = lax.axis_index('col')
    px, py = lax.rem(me, 2), me // 2
    peers = [py * 2 + (1 - px), (1 - py) * 2 + px, 3 - me]

    def rows_of(t):
        return pl.ds(pl.multiple_of(t * R, R), R)

    def lo_v(q):
        return jnp.maximum(q - 1, 0) // TB

    def z_remote(t, p):
        return pltpu.make_async_remote_copy(
            src_ref=z_hbm.at[:, pl.ds(pl.multiple_of(peers[p] * NL + t * R, R), R)],
            dst_ref=xT.at[pl.ds(pl.multiple_of(me * C, C), C), rows_of(t)],
            send_sem=z_send.at[t, p], recv_sem=z_recv.at[t, p],
            device_id=(peers[p], e), device_id_type=MESH)

    def z_local(t):
        return pltpu.make_async_copy(
            z_hbm.at[:, pl.ds(pl.multiple_of(me * NL + t * R, R), R)],
            xT.at[pl.ds(pl.multiple_of(me * C, C), C), rows_of(t)], z_loc.at[t])

    def v_remote(q, t):
        s = lax.rem(q, 2)
        return pltpu.make_async_remote_copy(
            src_ref=v_hbm.at[rows_of(t), pl.ds(pl.multiple_of(q * 128, 128), 128)],
            dst_ref=vst.at[s, e, rows_of(t), :],
            send_sem=v_send.at[s, t], recv_sem=v_recv.at[s, t],
            device_id=(me, 1 - e), device_id_type=MESH)

    def v_local(q, t):
        s = lax.rem(q, 2)
        return pltpu.make_async_copy(
            v_hbm.at[rows_of(t), pl.ds(pl.multiple_of(q * 128, 128), 128)],
            vst.at[s, e, rows_of(t), :], v_loc.at[s, t])

    def t_copy(q):
        return pltpu.make_async_copy(t_hbm.at[q], tb.at[lax.rem(q, 2)], t_sem.at[lax.rem(q, 2)])

    def rs_copy(c, p):
        return pltpu.make_async_remote_copy(
            src_ref=wsend.at[c, pl.ds(pl.multiple_of(peers[p] * SH, SH), SH), :],
            dst_ref=wrecv.at[c, p], send_sem=rs_send.at[c, p], recv_sem=rs_recv.at[c, p],
            device_id=(peers[p], e), device_id_type=MESH)

    def ag_copy(c, p):
        return pltpu.make_async_remote_copy(
            src_ref=ysend.at[c],
            dst_ref=yT.at[c, pl.ds(pl.multiple_of(me * SH, SH), SH), :],
            send_sem=ag_send.at[c, p], recv_sem=ag_recv.at[c, p],
            device_id=(peers[p], e), device_id_type=MESH)

    def v_fetch(q):
        def one(t, _):
            v_remote(q, t).start()
            v_local(q, t).start()
            return 0
        lax.fori_loop(lo_v(q), NT_TILES, one, 0)

    def v_sent(q):
        def one(t, _):
            v_remote(q, t).wait_send()
            return 0
        lax.fori_loop(lo_v(q), NT_TILES, one, 0)

    def prep_tile(q, t):
        s = lax.rem(q, 2)
        s3 = lax.rem(q, 3)
        v_local(q, t).wait()
        v_remote(q, t).wait_recv()
        rows = rows_of(t)
        for h in range(2):
            pieces = split3(vst[s, h, rows, :])
            for k in range(3):
                vb[s3, k, rows, h * 128:(h + 1) * 128] = pieces[k]

    def upd_tile(b, c, t, k):
        s3 = lax.rem(b, 3)
        rows = rows_of(t)
        cs = pl.ds(pl.multiple_of(c * C, C), C)
        p = dg(ysp[...], vb[s3, 0, rows, :], NT)
        q = dg(ysp[0:2 * C, :], vb[s3, 1, rows, :], NT)
        r = dg(ysp[0:C, :], vb[s3, 2, rows, :], NT)
        x = xT[cs, rows] - (p[0:C] + (p[C:2 * C] + q[0:C]) + (p[2 * C:] + q[C:] + r))
        xT[cs, rows] = x
        if k is not None:
            for i, piece in enumerate(split3(x)):
                xs[k, i * C:(i + 1) * C, :] = piece

    def w_tile(q, t, k):
        s3 = lax.rem(q, 3)
        rows = rows_of(t)
        p = dg(xs[k], vb[s3, 0, rows, :], NN)
        u = dg(xs[k, 0:2 * C], vb[s3, 1, rows, :], NN)
        r = dg(xs[k, 0:C], vb[s3, 2, rows, :], NN)
        wacc[...] += p[0:C] + (p[C:2 * C] + u[0:C]) + (p[2 * C:] + u[C:] + r)

    def w_send(c):
        wsend[c] = wacc[...]
        for p in range(3):
            rs_copy(c, p).start()

    def rs_handle(j):
        c = lax.rem(j, 4)
        q = NB - 1 - j // 4
        for p in range(3):
            rs_copy(c, p).wait_recv()
        mine = pl.ds(pl.multiple_of(me * SH, SH), SH)
        w = (wsend[c, mine, :] + wrecv[c, 0]) + (wrecv[c, 1] + wrecv[c, 2])
        y = lax.dot_general(w, tb[lax.rem(q, 2)], NT, precision=HIGHEST, preferred_element_type=F32)
        ysend[c] = y
        yT[c, mine, :] = y
        for p in range(3):
            ag_copy(c, p).start()

    def ag_wait(c):
        for p in range(3):
            ag_copy(c, p).wait_recv()
        for i, piece in enumerate(split3(yT[c])):
            ysp[i * C:(i + 1) * C, :] = piece

    def z_wait(t):
        z_local(t).wait()
        for p in range(3):
            z_remote(t, p).wait_recv()

    barrier = pltpu.get_barrier_semaphore()
    for p in range(3):
        pl.semaphore_signal(barrier, inc=1, device_id=(peers[p], e), device_id_type=MESH)
    pl.semaphore_signal(barrier, inc=1, device_id=(me, 1 - e), device_id_type=MESH)
    pl.semaphore_wait(barrier, 4)

    v_fetch(NB - 1)
    v_fetch(NB - 2)
    t_copy(NB - 1).start()
    t_copy(NB - 2).start()

    def z_start(n, _):
        t = NT_TILES - 1 - n
        for p in range(3):
            z_remote(t, p).start()
        z_local(t).start()
        return 0
    lax.fori_loop(0, NT_TILES, z_start, 0)

    def prep_all(q):
        def one(t, _):
            prep_tile(q, t)
            return 0
        lax.fori_loop(lo_v(q), NT_TILES, one, 0)

    def v_release(q):
        pl.semaphore_signal(vfree, inc=1, device_id=(me, 1 - e), device_id_type=MESH)
        v_sent(q)
        pl.semaphore_wait(vfree, 1)
        v_fetch(q - 2)

    prep_all(NB - 1)
    v_release(NB - 1)
    prep_all(NB - 2)
    v_release(NB - 2)

    last = NT_TILES - 1
    z_wait(last)
    t_copy(NB - 1).wait()

    def first_w(c, _):
        cs = pl.ds(pl.multiple_of(c * C, C), C)
        for i, piece in enumerate(split3(xT[cs, last * R:(last + 1) * R])):
            xs[0, i * C:(i + 1) * C, :] = piece
        wacc[...] = jnp.zeros_like(wacc)
        w_tile(NB - 1, last, 0)
        w_send(c)
        return 0
    lax.fori_loop(0, 4, first_w, 0)
    rs_handle(0)
    rs_handle(1)

    def slot(i, _):
        b = NB - 1 - i // 4
        c = lax.rem(i, 4)

        @pl.when(jnp.logical_and(c == 0, lax.rem(b, TB) == 0))
        def _():
            z_wait((b - 1) // TB)

        @pl.when(jnp.logical_and(c == 2, b >= 1))
        def _():
            t_copy(b - 1).wait()

            @pl.when(b >= 2)
            def _():
                t_copy(b - 2).start()

        for p in range(3):
            ag_copy(c, p).wait_send()
        ag_wait(c)
        wacc[...] = jnp.zeros_like(wacc)
        lo = (b - 1) // TB
        upd_tile(b, c, lo, lax.rem(lo, 2))

        def tile(t, _):
            w_tile(b - 1, t - 1, lax.rem(t - 1, 2))
            upd_tile(b, c, t, lax.rem(t, 2))
            return 0
        lax.fori_loop(lo + 1, NT_TILES, tile, 0)
        rs_handle(i + 2)
        w_tile(b - 1, last, last % 2)
        for p in range(3):
            rs_copy(c, p).wait_send()
        w_send(c)

        @pl.when(b >= 2)
        def _():
            q = b - 2
            for h in range((NT_TILES + 3) // 4):
                t = c + 4 * h

                @pl.when(jnp.logical_and(t >= lo_v(q), t < NT_TILES))
                def _():
                    prep_tile(q, t)

            @pl.when(jnp.logical_and(c == 3, q >= 2))
            def _():
                v_release(q)
        return 0

    lax.fori_loop(0, 4 * (NB - 1), slot, 0)

    def end_slot(c, _):
        for p in range(3):
            ag_copy(c, p).wait_send()
            rs_copy(c, p).wait_send()
        ag_wait(c)

        def tile(t, _):
            upd_tile(0, c, t, None)
            return 0
        lax.fori_loop(0, NT_TILES, tile, 0)
        cs = pl.ds(pl.multiple_of(c * C, C), C)
        pltpu.make_async_copy(xT.at[cs, :], out_hbm.at[cs, :], o_sem.at[c]).start()

        @pl.when(c < 2)
        def _():
            rs_handle(4 * (NB - 1) + c + 2)
        return 0
    lax.fori_loop(0, 4, end_slot, 0)

    for c in range(4):
        cs = pl.ds(c * C, C)
        pltpu.make_async_copy(xT.at[cs, :], out_hbm.at[cs, :], o_sem.at[c]).wait()

    def z_sent(t, _):
        for p in range(3):
            z_remote(t, p).wait_send()
        return 0
    lax.fori_loop(0, NT_TILES, z_sent, 0)
    v_sent(1)
    v_sent(0)


def solution(mesh):
    def local_apply(v_loc, t_loc, z_loc):
        NL, half = v_loc.shape
        NB = half // 128
        R = min(512, NL // 4)
        tiles = NL // R
        e = lax.axis_index('col')
        other = lax.ppermute(v_loc, 'col', [(0, 1), (1, 0)])
        v0 = jnp.where(e == 0, v_loc, other).reshape(NL, NB, 128)
        v1 = jnp.where(e == 0, other, v_loc).reshape(NL, NB, 128)
        gram = lax.psum(jnp.einsum('rla,rlb->lab', v0, v1, precision=HIGHEST), 'row')
        t_all = lax.all_gather(t_loc, 'col', axis=0)
        t01 = -jnp.einsum('lab,lbc,lcd->lad', t_all[0], gram, t_all[1], precision=HIGHEST)
        t_pair = jnp.concatenate([
            jnp.concatenate([t_all[0], t01], axis=2),
            jnp.concatenate([jnp.zeros_like(t01), t_all[1]], axis=2)], axis=1)
        z_t = z_loc.T
        any_ = pl.BlockSpec(memory_space=pl.ANY)
        dma = pltpu.SemaphoreType.DMA
        x_t = pl.pallas_call(
            functools.partial(kernel, R, NB),
            out_shape=jax.ShapeDtypeStruct((4 * C, NL), F32),
            in_specs=[any_] * 3,
            out_specs=any_,
            scratch_shapes=[
                pltpu.VMEM((4 * C, NL), F32),
                pltpu.VMEM((2, 2, NL, 128), F32),
                pltpu.VMEM((3, 3, NL, B), BF16),
                pltpu.VMEM((2, B, B), F32),
                pltpu.VMEM((3 * C, B), BF16),
                pltpu.VMEM((2, 3 * C, R), BF16),
                pltpu.VMEM((C, B), F32),
                pltpu.VMEM((4, C, B), F32),
                pltpu.VMEM((4, 3, SH, B), F32),
                pltpu.VMEM((4, SH, B), F32),
                pltpu.VMEM((4, C, B), F32),
                dma((tiles, 3)), dma((tiles, 3)), dma((tiles,)),
                dma((2, tiles)), dma((2, tiles)), dma((2, tiles)), dma((2,)),
                dma((4, 3)), dma((4, 3)), dma((4, 3)), dma((4, 3)), dma((4,)),
                pltpu.SemaphoreType.REGULAR,
            ],
            compiler_params=pltpu.CompilerParams(
                collective_id=0, has_side_effects=True, vmem_limit_bytes=62 * 1024 * 1024),
            name='back_transform',
        )(t_pair, v_loc, z_t)
        return x_t.T

    return jax.shard_map(local_apply, mesh=mesh,
                         in_specs=(P('row', 'col'), P('col', None, None), P(None, ('col', 'row'))),
                         out_specs=P('row', 'col'), check_vma=False)
```

time: 8130 us -> 2010 us (0.25)
  waiting for transfers between devices: 4780 us -> 276 us
  matrix products: 2930 us -> 162 us
  Pallas kernels: 0 us -> 1220 us
  other arithmetic: 0 us -> 176 us
  blocking collectives: 121 us -> 0 us
  local copies, waits for them, and re-layouts: 268 us -> 157 us
    psum x128 -> x1, waiting for transfers between devices: 4130 us -> 77.4 us  [local_apply(): lax.psum(jnp.einsum('rla,rlb->lab', v0, v1, precision=HIGHEST), 'row')]
    dot_general x384 -> x3, matrix products: 2930 us -> 162 us  [the longest x1 144 us: local_apply(): jnp.einsum('rla,rlb->lab', v0, v1, precision=HIGHEST)]
    pallas_call x0 -> x1, Pallas kernels: none -> 1220 us  [local_apply(): pl.pallas_call(functools.partial(kernel, R, NB), out_shape=jax.ShapeDtype...]
    all_gather x64 -> x1, waiting for transfers between devices: 552 us -> 0.01 us  [local_apply(): t_all = lax.all_gather(t_loc, 'col', axis=0)]
    dynamic_slice x128 -> x0, local copies, waits for them, and re-layouts: 250 us -> none  [the longest x64 195 us: group_step(): lax.dynamic_slice_in_dim(v_loc, group_idx * panel_width, panel_width, axi...]
    ppermute x0 -> x1, waiting for transfers between devices: none -> 199 us  [local_apply(): other = lax.ppermute(v_loc, 'col', [(0, 1), (1, 0)])]
    unnamed x0 -> x1, other arithmetic: none -> 170 us
    reshape x0 -> x1, local copies, waits for them, and re-layouts: none -> 131 us  [local_apply(): v0 = jnp.where(e == 0, v_loc, other).reshape(NL, NB, 128)]
  transfers between devices with their start and end apart: 193 -> 3, of which waited for: 193 -> 2; matrix products, arithmetic and copies ran while one was open for 1% -> 23% of each run, Pallas kernels for 0% -> 0%
where the time goes in v1:
time: 2010 us
  Pallas kernels  1220 us (61%)
  waiting for transfers between devices  276 us (14%)
  other arithmetic  176 us (9%)
  matrix products  162 us (8%)
  local copies, waits for them, and re-layouts  157 us (8%)
    pallas_call x1, Pallas kernels, local_apply(): pl.pallas_call(functools.partial(kernel, R, NB), out_shape=jax.ShapeDtype...  1220 us
    ppermute x1, waiting for transfers between devices, local_apply(): other = lax.ppermute(v_loc, 'col', [(0, 1), (1, 0)])  199 us
    unnamed x1, other arithmetic  170 us
    dot_general x1, matrix products, local_apply(): jnp.einsum('rla,rlb->lab', v0, v1, precision=HIGHEST)  144 us
    reshape x1, local copies, waits for them, and re-layouts, local_apply(): v0 = jnp.where(e == 0, v_loc, other).reshape(NL, NB, 128)  131 us
    psum x1, waiting for transfers between devices, local_apply(): lax.psum(jnp.einsum('rla,rlb->lab', v0, v1, precision=HIGHEST), 'row')  77.4 us
  transfers between devices with their start and end apart: 3, of which 2 were waited for; matrix products, arithmetic and copies ran while one was open for 23% of the time, Pallas kernels for 0%

profile of v1, /device:TPU:0, one launch (start us, length us, event | category | flops | bytes accessed | tf_op | source)
XLA Modules:
  0.0 2011.3 jit_solution(5304234318414546532)
XLA Ops:
  7.4 0.0 all-gather.3.cloned.1.call-start
  7.4 0.9 collective-permute-start
  8.2 0.0 all-gather.3.cloned.1.call-update
  8.3 0.0 all-reduce.3.cloned.1.call-start
  8.3 198.7 %collective-permute-done = f32[4096,8192]{1,0:T(8,128)} collective-permute-done((f32[4096,8192]{1,0:T(8,128)}, f32[4096,8192]{1,0:T(8,128)}, u32[]{:S(2)}, u32[]{:S(2)}) %collective-permute-start) | collective-permute-done | bytes 134217760 | tf_op jit(solution)/shard_map/ppermute | solution.py:309
  207.0 169.7 %select_bitcast_fusion = (f32[512,64,8,128]{3,2,1,0:T(8,128)}, f32[4096,8192]{1,0:T(8,128)}) fusion(f32[4096,8192]{1,0:T(8,128)} %collective-permute-done, f32[4096,8192]{1,0:T(8,128)} %v_hbm.1, pred[]{:T(512)S(6)} %eq.4), kind=kLoop, calls=%fused_computation.3 | loop fusion | flops 67108864 | bytes 536870912
  376.6 131.3 %copy.16 = f32[4096,8192]{0,1:T(8,128)} copy(f32[4096,8192]{1,0:T(8,128)} %get-tuple-element.6) | data formatting | bytes 268435456 | tf_op jit(solution)/shard_map/reshape | solution.py:310
  508.0 144.0 %fusion = f32[64,128,128]{2,1,0:T(8,128)} fusion(f32[4096,64,128]{0,2,1:T(8,128)} %bitcast, f32[512,64,8,128]{3,2,1,0:T(8,128)} %get-tuple-element.5), kind=kOutput, calls=%fused_computation | convolution fusion | flops 51539607552 | bytes 272629760 | tf_op jit(solution)/shard_map/rla,rlb->lab/dot_general | solution.py:312
  651.9 0.0 all-reduce.3.cloned.1.call-update
  652.0 9.0 copy.10
  661.0 0.0 all-gather.3.cloned.1.call-done
  661.0 7.8 fusion.6
  668.8 77.4 %all-reduce.3.cloned.1.call-done = f32[64,128,128]{2,1,0:T(8,128)} async-done(((f32[64,128,128]{2,1,0:T(8,128)}), f32[64,128,128]{2,1,0:T(8,128)}) %all-reduce.3.cloned.1.call-update) | async-done | bytes 4194320 | tf_op jit(solution)/shard_map/psum | solution.py:312
  746.2 0.0 copy-start
  746.2 10.5 fusion.4
  756.7 0.0 copy-done
  756.7 0.0 copy-start.1
  756.7 0.0 copy-start.2
  756.7 7.3 convolution_negate_fusion
  764.0 0.0 copy-done.1
  764.0 0.0 copy-done.2
  764.0 6.2 select_maximum_fusion.t_hbm
  770.2 1224.8 %back_transform.1 = f32[512,4096]{1,0:T(8,128)} custom-call(f32[64,256,256]{2,1,0:T(8,128)} %select_maximum_fusion.t_hbm, f32[4096,8192]{1,0:T(8,128)} %v_hbm.1, f32[128,16384]{1,0:T(8,128)} %bitcast.11), custom_call_target="tpu_custom_call" | custom-call | tf_op jit(solution)/shard_map/back_transform/pallas_call | solution.py:321
  1994.9 8.9 copy.11
Async XLA Ops:
  7.4 653.6 %all-gather.3.cloned.1.call-start = ((), (), s32[]{:S(2)}) async-start(), calls=%async_computation.1 | async-start | bytes 12582912 | tf_op jit(solution)/shard_map/all_gather | solution.py:313
  7.4 199.6 %collective-permute-start = (f32[4096,8192]{1,0:T(8,128)}, f32[4096,8192]{1,0:T(8,128)}, u32[]{:S(2)}, u32[]{:S(2)}) collective-permute-start(f32[4096,8192]{1,0:T(8,128)} %v_hbm.1), channel_id=1, source_target_pairs={{0,1},{1,0},{2,3},{3,2},{4,5},{5,4},{6,7},{7,6}} | collective-permute-start | bytes 402653184 | tf_op jit(solution)/shard_map/ppermute | solution.py:309
  8.3 737.9 %all-reduce.3.cloned.1.call-start = ((), (), s32[]{:S(2)}) async-start(), calls=%async_computation | async-start | bytes 8388608 | tf_op jit(solution)/shard_map/psum | solution.py:312
  746.2 10.5 copy-start
  756.7 7.3 copy-start.1
  756.7 7.3 copy-start.2
Sparse Core Ops, SparseCore 0:
  9.7 26.1 all-gather.2
Sparse Core Ops, SparseCore 1:
  652.1 94.1 all-reduce.2

commit v2 on v0

v2 whole, which is shorter than its diff:
```python
import functools

import jax
import jax.numpy as jnp
from jax import lax
from jax.experimental import pallas as pl
from jax.experimental.pallas import tpu as pltpu
from jax.sharding import PartitionSpec as P

HIGHEST = lax.Precision.HIGHEST
F32 = jnp.float32
BF16 = jnp.bfloat16
MESH = pl.DeviceIdType.MESH
NN = (((1,), (0,)), ((), ()))
NT = (((1,), (1,)), ((), ()))
C = 128
B = 256
SH = 32


def dg(a, b, dims=NN):
    return lax.dot_general(a, b, dims, preferred_element_type=F32)


def split3(x):
    x0 = x.astype(BF16)
    r1 = x - x0.astype(F32)
    x1 = r1.astype(BF16)
    x2 = (r1 - x1.astype(F32)).astype(BF16)
    return x0, x1, x2


def dot6(m, stack, b0, b1, b2, dims=NN):
    p = dg(stack[0:3 * m], b0, dims)
    q = dg(stack[0:2 * m], b1, dims)
    r = dg(stack[0:m], b2, dims)
    return p[0:m] + (p[m:2 * m] + q[0:m]) + (p[2 * m:] + q[m:] + r)


def kernel(R, NB, t_hbm, v_hbm, z_hbm, out_hbm,
           xT, vst, vb, tst, tp, ysp, xsa, xsb, wacc, wsend, wrecv, ysend, yT,
           gacc, gsend, grecv, gown, gfull, t01s, t01r,
           z_send, z_recv, z_loc, v_send, v_recv, v_loc, t_send, t_recv, t_loc,
           rs_send, rs_recv, ag_send, ag_recv, g_sems, p_send, p_recv, o_sem, vfree):
    NL = xT.shape[1]
    NTL = NL // R
    TB = R // 64
    H = R // 2
    G = R // 4
    ZP = R // 128
    me = lax.axis_index('row')
    e = lax.axis_index('col')
    px, py = lax.rem(me, 2), me // 2
    peers = [py * 2 + (1 - px), (1 - py) * 2 + px, 3 - me]
    mine = pl.ds(pl.multiple_of(me * SH, SH), SH)

    def rows_of(t):
        return pl.ds(pl.multiple_of(t * R, R), R)

    def chunk(c):
        return pl.ds(pl.multiple_of(c * C, C), C)

    def lo_v(q):
        return jnp.maximum(q - 1, 0) // TB

    def own(q):
        return lax.rem(q, 2) == e

    def z_remote(k, p):
        return pltpu.make_async_remote_copy(
            src_ref=z_hbm.at[:, pl.ds(pl.multiple_of(peers[p] * NL + k * 128, 128), 128)],
            dst_ref=xT.at[chunk(me), pl.ds(pl.multiple_of(k * 128, 128), 128)],
            send_sem=z_send.at[k, p], recv_sem=z_recv.at[k, p],
            device_id=(peers[p], e), device_id_type=MESH)

    def z_local(k):
        return pltpu.make_async_copy(
            z_hbm.at[:, pl.ds(pl.multiple_of(me * NL + k * 128, 128), 128)],
            xT.at[chunk(me), pl.ds(pl.multiple_of(k * 128, 128), 128)], z_loc.at[k])

    def v_remote(q, t):
        s = lax.rem(q, 2)
        return pltpu.make_async_remote_copy(
            src_ref=v_hbm.at[rows_of(t), pl.ds(pl.multiple_of(q * 128, 128), 128)],
            dst_ref=vst.at[s, e, rows_of(t), :],
            send_sem=v_send.at[s, t], recv_sem=v_recv.at[s, t],
            device_id=(me, 1 - e), device_id_type=MESH)

    def v_local(q, t):
        s = lax.rem(q, 2)
        return pltpu.make_async_copy(
            v_hbm.at[rows_of(t), pl.ds(pl.multiple_of(q * 128, 128), 128)],
            vst.at[s, e, rows_of(t), :], v_loc.at[s, t])

    def t_remote(q):
        s = lax.rem(q, 4)
        return pltpu.make_async_remote_copy(
            src_ref=t_hbm.at[q], dst_ref=tst.at[s, e], send_sem=t_send.at[s], recv_sem=t_recv.at[s],
            device_id=(me, 1 - e), device_id_type=MESH)

    def t_local(q):
        s = lax.rem(q, 4)
        return pltpu.make_async_copy(t_hbm.at[q], tst.at[s, e], t_loc.at[s])

    def t01_copy(q):
        s = lax.rem(q // 2, 2)
        return pltpu.make_async_remote_copy(
            src_ref=t01s.at[s], dst_ref=t01r.at[s], send_sem=p_send.at[s], recv_sem=p_recv.at[s],
            device_id=(me, 1 - e), device_id_type=MESH)

    def rs_copy(c, p):
        return pltpu.make_async_remote_copy(
            src_ref=wsend.at[c, pl.ds(pl.multiple_of(peers[p] * SH, SH), SH), :],
            dst_ref=wrecv.at[c, p], send_sem=rs_send.at[c, p], recv_sem=rs_recv.at[c, p],
            device_id=(peers[p], e), device_id_type=MESH)

    def ag_copy(c, p):
        return pltpu.make_async_remote_copy(
            src_ref=ysend.at[c], dst_ref=yT.at[c, mine, :],
            send_sem=ag_send.at[c, p], recv_sem=ag_recv.at[c, p],
            device_id=(peers[p], e), device_id_type=MESH)

    def grs_copy(p):
        return pltpu.make_async_remote_copy(
            src_ref=gsend.at[pl.ds(pl.multiple_of(peers[p] * SH, SH), SH), :],
            dst_ref=grecv.at[p], send_sem=g_sems.at[0, p], recv_sem=g_sems.at[1, p],
            device_id=(peers[p], e), device_id_type=MESH)

    def gag_copy(p):
        return pltpu.make_async_remote_copy(
            src_ref=gown, dst_ref=gfull.at[mine, :], send_sem=g_sems.at[2, p], recv_sem=g_sems.at[3, p],
            device_id=(peers[p], e), device_id_type=MESH)

    def over_tiles(q, fn):
        def one(t, _):
            fn(q, t)
            return 0
        lax.fori_loop(lo_v(q), NTL, one, 0)

    def fetch(q):
        def one(q, t):
            v_remote(q, t).start()
            v_local(q, t).start()
        over_tiles(q, one)
        t_remote(q).start()
        t_local(q).start()

    def arrived(q):
        def one(q, t):
            v_local(q, t).wait()
            v_remote(q, t).wait_recv()
        over_tiles(q, one)
        t_local(q).wait()
        t_remote(q).wait_recv()

    def sent(q):
        over_tiles(q, lambda q, t: v_remote(q, t).wait_send())
        t_remote(q).wait_send()

    def release(q):
        pl.semaphore_signal(vfree, inc=1, device_id=(me, 1 - e), device_id_type=MESH)
        sent(q)
        pl.semaphore_wait(vfree, 1)
        fetch(q - 2)

    def prep(q, r0, gram):
        s, s4 = lax.rem(q, 2), lax.rem(q, 4)
        rows = pl.ds(pl.multiple_of(r0, G), G)
        f0, f1 = vst[s, 0, rows, :], vst[s, 1, rows, :]
        p0, p1 = split3(f0), split3(f1)
        for k in range(3):
            vb[s4, k, rows, 0:128] = p0[k]
            vb[s4, k, rows, 128:256] = p1[k]
        if gram:
            gacc[...] += dot6(128, jnp.concatenate(split3(f0.T), axis=0), *p1)

    def g_start(q):
        gsend[...] = gacc[...]
        for p in range(3):
            grs_copy(p).start()

    def g_mid(q):
        for p in range(3):
            grs_copy(p).wait_recv()
        g = (gsend[mine, :] + grecv[0]) + (grecv[1] + grecv[2])
        gown[...] = g
        gfull[mine, :] = g
        for p in range(3):
            gag_copy(p).start()

    def g_fin(q):
        for p in range(3):
            gag_copy(p).wait_recv()
            grs_copy(p).wait_send()
            gag_copy(p).wait_send()
        s = lax.rem(q, 4)
        u = lax.dot_general(tst[s, 0], gfull[...], NN, precision=HIGHEST, preferred_element_type=F32)
        t01 = -lax.dot_general(u, tst[s, 1], NN, precision=HIGHEST, preferred_element_type=F32)
        t01s[lax.rem(q // 2, 2)] = t01
        t01_copy(q).start()

    def t_build(q):
        s, s2, sh = lax.rem(q, 4), lax.rem(q, 2), lax.rem(q // 2, 2)

        def put(t01):
            tt = jnp.concatenate([
                jnp.concatenate([tst[s, 0].T, jnp.zeros((128, 128), F32)], axis=1),
                jnp.concatenate([t01.T, tst[s, 1].T], axis=1)], axis=0)
            for k, piece in enumerate(split3(tt)):
                tp[s2, k] = piece

        @pl.when(own(q))
        def _():
            t01_copy(q).wait_send()
            put(t01s[sh])

        @pl.when(jnp.logical_not(own(q)))
        def _():
            t01_copy(q).wait_recv()
            put(t01r[sh])

    def upd(b, c, r0, xs):
        s4 = lax.rem(b, 4)
        rows = pl.ds(pl.multiple_of(r0, H), H)
        d = dot6(C, ysp[...], vb[s4, 0, rows, :], vb[s4, 1, rows, :], vb[s4, 2, rows, :], NT)
        x = xT[chunk(c), rows] - d
        xT[chunk(c), rows] = x
        if xs is not None:
            for i, piece in enumerate(split3(x)):
                xs[i * C:(i + 1) * C, :] = piece

    def wprod(q, r0, xs):
        s4 = lax.rem(q, 4)
        rows = pl.ds(pl.multiple_of(r0, H), H)
        return dot6(C, xs[...], vb[s4, 0, rows, :], vb[s4, 1, rows, :], vb[s4, 2, rows, :])

    def body(b, c, t, first, gram):
        lo = (b - 1) // TB
        q = jnp.maximum(b - 3, 0)
        ra = t * R
        upd(b, c, ra, xsa)
        prep(q, lo * R + (c * (NTL - lo) + (t - lo)) * G, gram)
        w = None if first else wprod(b - 1, ra - H, xsb)
        upd(b, c, ra + H, xsb)
        if first:
            wacc[...] = wprod(b - 1, ra, xsa)
        else:
            wacc[...] += w + wprod(b - 1, ra, xsa)

    def rs_wait(j):
        for p in range(3):
            rs_copy(lax.rem(j, 4), p).wait_recv()

    def rs_sum(j):
        c = lax.rem(j, 4)
        s2 = lax.rem(NB - 1 - j // 4, 2)
        w = (wsend[c, mine, :] + wrecv[c, 0]) + (wrecv[c, 1] + wrecv[c, 2])
        y = dot6(SH, jnp.concatenate(split3(w), axis=0), tp[s2, 0], tp[s2, 1], tp[s2, 2])
        ysend[c] = y
        yT[c, mine, :] = y

    def y_send(j):
        for p in range(3):
            ag_copy(lax.rem(j, 4), p).start()

    def w_send(c):
        for p in range(3):
            rs_copy(c, p).start()

    def y_take(c):
        for p in range(3):
            ag_copy(c, p).wait_recv()
            ag_copy(c, p).wait_send()
            rs_copy(c, p).wait_send()
        for i, piece in enumerate(split3(yT[c])):
            ysp[i * C:(i + 1) * C, :] = piece

    def z_start(k):
        for p in range(3):
            z_remote(k, p).start()
        z_local(k).start()

    def z_wait(t):
        def one(k, _):
            z_local(k).wait()
            for p in range(3):
                z_remote(k, p).wait_recv()
            return 0
        lax.fori_loop(t * ZP, (t + 1) * ZP, one, 0)

    barrier = pltpu.get_barrier_semaphore()
    for p in range(3):
        pl.semaphore_signal(barrier, inc=1, device_id=(peers[p], e), device_id_type=MESH)
    pl.semaphore_signal(barrier, inc=1, device_id=(me, 1 - e), device_id_type=MESH)
    pl.semaphore_wait(barrier, 4)

    fetch(NB - 1)
    fetch(NB - 2)

    def z_first(n, _):
        z_start(NTL * ZP - 1 - n)
        return 0
    lax.fori_loop(0, ZP, z_first, 0)

    def prep_all(q):
        arrived(q)

        def one(n, _):
            prep(q, lo_v(q) * R + n * G, True)
            return 0

        gacc[...] = jnp.zeros_like(gacc)
        lax.fori_loop(0, 4 * (NTL - lo_v(q)), one, 0)

    def when_own(q, fn):
        @pl.when(own(q))
        def _():
            fn(q)

    prep_all(NB - 1)
    when_own(NB - 1, g_start)
    release(NB - 1)
    prep_all(NB - 2)
    when_own(NB - 2, g_start)
    release(NB - 2)
    when_own(NB - 1, g_mid)
    when_own(NB - 2, g_mid)
    when_own(NB - 1, g_fin)
    when_own(NB - 2, g_fin)
    prep_all(NB - 3)
    when_own(NB - 3, g_start)
    t_build(NB - 1)
    release(NB - 3)
    z_wait(NTL - 1)

    def first_w(c, _):
        base = (NTL - 1) * R
        for n, xs in enumerate((xsa, xsb)):
            for i, piece in enumerate(split3(xT[chunk(c), base + n * H:base + (n + 1) * H])):
                xs[i * C:(i + 1) * C, :] = piece
        wsend[c] = wprod(NB - 1, base, xsa) + wprod(NB - 1, base + H, xsb)
        w_send(c)
        return 0
    lax.fori_loop(0, 4, first_w, 0)
    for j in range(2):
        rs_wait(j)
        rs_sum(j)
        y_send(j)

    def slot(i, _):
        b = NB - 1 - i // 4
        c = lax.rem(i, 4)
        lo = (b - 1) // TB
        q3 = b - 3

        @pl.when(c == 0)
        def _():
            @pl.when(lax.rem(b, TB) == 0)
            def _():
                z_wait(lo)

            @pl.when(jnp.logical_and(lo >= 1, lax.rem(TB * (lo + 1) - 1 - b, TB // ZP) == 0))
            def _():
                z_start((lo - 1) * ZP + ZP - 1 - (TB * (lo + 1) - 1 - b) // (TB // ZP))

            @pl.when(q3 >= 0)
            def _():
                arrived(q3)
                gacc[...] = jnp.zeros_like(gacc)

        @pl.when(c == 1)
        def _():
            @pl.when(jnp.logical_and(own(b - 2), b >= 2))
            def _():
                g_mid(b - 2)
            t_build(b - 1)

        @pl.when(jnp.logical_and(q3 >= 0, lo_v(q3) < lo))
        def _():
            @pl.when(own(q3))
            def _():
                prep(q3, lo_v(q3) * R + c * G, True)

            @pl.when(jnp.logical_not(own(q3)))
            def _():
                prep(q3, lo_v(q3) * R + c * G, False)

        def run(gram):
            y_take(c)
            body(b, c, lo, True, gram)

            def tile(t, _):
                body(b, c, t, False, gram)
                return 0
            lax.fori_loop(lo + 1, NTL, tile, 0)

        with_gram = jnp.logical_and(q3 >= 0, own(q3))

        @pl.when(with_gram)
        def _():
            run(True)

        @pl.when(jnp.logical_not(with_gram))
        def _():
            run(False)

        rs_wait(i + 2)
        rs_sum(i + 2)
        wsend[c] = wacc[...] + wprod(b - 1, NL - H, xsb)
        y_send(i + 2)
        w_send(c)

        @pl.when(c == 3)
        def _():
            @pl.when(jnp.logical_and(own(b - 2), b >= 2))
            def _():
                g_fin(b - 2)

            @pl.when(with_gram)
            def _():
                g_start(q3)

            @pl.when(q3 >= 2)
            def _():
                release(q3)
        return 0

    lax.fori_loop(0, 4 * (NB - 1), slot, 0)

    def out_copy(c):
        return pltpu.make_async_copy(xT.at[chunk(c), :], out_hbm.at[chunk(c), :], o_sem.at[c])

    def end_slot(c, _):
        @pl.when(c < 2)
        def _():
            j = 4 * (NB - 1) + c + 2
            rs_wait(j)
            rs_sum(j)
            y_send(j)
        y_take(c)

        def tile(t, _):
            upd(0, c, t * R, None)
            upd(0, c, t * R + H, None)
            return 0
        lax.fori_loop(0, NTL, tile, 0)
        out_copy(c).start()
        return 0
    lax.fori_loop(0, 4, end_slot, 0)

    for c in range(4):
        out_copy(c).wait()

    def z_sent(k, _):
        for p in range(3):
            z_remote(k, p).wait_send()
        return 0
    lax.fori_loop(0, NTL * ZP, z_sent, 0)
    sent(1)
    sent(0)


def solution(mesh):
    def local_apply(v_loc, t_loc, z_loc):
        NL, half = v_loc.shape
        NB = half // 128
        R = min(1024, NL // 2)
        tiles = NL // R
        H = R // 2
        z_t = z_loc.T
        any_ = pl.BlockSpec(memory_space=pl.ANY)
        dma = pltpu.SemaphoreType.DMA
        vmem = pltpu.VMEM
        x_t = pl.pallas_call(
            functools.partial(kernel, R, NB),
            out_shape=jax.ShapeDtypeStruct((4 * C, NL), F32),
            in_specs=[any_] * 3,
            out_specs=any_,
            scratch_shapes=[
                vmem((4 * C, NL), F32),
                vmem((2, 2, NL, 128), F32),
                vmem((4, 3, NL, B), BF16),
                vmem((4, 2, 128, 128), F32),
                vmem((2, 3, B, B), BF16),
                vmem((3 * C, B), BF16),
                vmem((3 * C, H), BF16),
                vmem((3 * C, H), BF16),
                vmem((C, B), F32),
                vmem((4, C, B), F32),
                vmem((4, 3, SH, B), F32),
                vmem((4, SH, B), F32),
                vmem((4, C, B), F32),
                vmem((128, 128), F32),
                vmem((128, 128), F32),
                vmem((3, SH, 128), F32),
                vmem((SH, 128), F32),
                vmem((128, 128), F32),
                vmem((2, 128, 128), F32),
                vmem((2, 128, 128), F32),
                dma((NL // 128, 3)), dma((NL // 128, 3)), dma((NL // 128,)),
                dma((2, tiles)), dma((2, tiles)), dma((2, tiles)),
                dma((4,)), dma((4,)), dma((4,)),
                dma((4, 3)), dma((4, 3)), dma((4, 3)), dma((4, 3)),
                dma((4, 3)), dma((2,)), dma((2,)), dma((4,)),
                pltpu.SemaphoreType.REGULAR,
            ],
            compiler_params=pltpu.CompilerParams(
                collective_id=0, has_side_effects=True, vmem_limit_bytes=62 * 1024 * 1024),
            name='back_transform',
        )(t_loc, v_loc, z_t)
        return x_t.T

    return jax.shard_map(local_apply, mesh=mesh,
                         in_specs=(P('row', 'col'), P('col', None, None), P(None, ('col', 'row'))),
                         out_specs=P('row', 'col'), check_vma=False)
```

time: 8130 us -> 1140 us (0.14)
  waiting for transfers between devices: 4780 us -> 0 us
  matrix products: 2930 us -> 0 us
  Pallas kernels: 0 us -> 1120 us
  local copies, waits for them, and re-layouts: 268 us -> 17.9 us
  blocking collectives: 121 us -> 0 us
    psum x128 -> x0, waiting for transfers between devices: 4130 us -> none  [panel_step(): w_full = lax.psum(w_part, 'row')]
    dot_general x384 -> x0, matrix products: 2930 us -> none  [the longest x128 1510 us: panel_step(): jnp.dot(v_j, y_mat, precision=HIGHEST, preferred_element_type=jnp.float32)]
    pallas_call x0 -> x1, Pallas kernels: none -> 1120 us  [local_apply(): pl.pallas_call(functools.partial(kernel, R, NB), out_shape=jax.ShapeDtype...]
    all_gather x64 -> x0, waiting for transfers between devices: 552 us -> none  [group_step(): v_group = lax.all_gather(v_blk, 'col', axis=0)]
    dynamic_slice x128 -> x0, local copies, waits for them, and re-layouts: 250 us -> none  [the longest x64 195 us: group_step(): lax.dynamic_slice_in_dim(v_loc, group_idx * panel_width, panel_width, axi...]
    all_gather x64 -> x0, blocking collectives: 121 us -> none  [group_step(): t_group = lax.all_gather(t_blk, 'col', axis=0)]
    all_to_all x1 -> x0, waiting for transfers between devices: 94 us -> none  [local_apply(): x_loc = lax.all_to_all(z_loc, 'row', 0, 1, tiled=True)]
  transfers between devices with their start and end apart: 193 -> 0, of which waited for: 193 -> 0; matrix products, arithmetic and copies ran while one was open for 1% -> 0% of each run, Pallas kernels for 0% -> 0%
where the time goes in v2:
time: 1140 us
  Pallas kernels  1120 us (98%)
  local copies, waits for them, and re-layouts  17.9 us (2%)
    pallas_call x1, Pallas kernels, local_apply(): pl.pallas_call(functools.partial(kernel, R, NB), out_shape=jax.ShapeDtype...  1120 us

profile of v2, /device:TPU:0, one launch (start us, length us, event | category | flops | bytes accessed | tf_op | source)
XLA Modules:
  0.0 1135.5 jit_solution(8256433666019314916)
XLA Ops:
  0.0 9.0 copy.4
  9.0 1117.6 %back_transform.1 = f32[512,4096]{1,0:T(8,128)} custom-call(f32[64,128,128]{2,1,0:T(8,128)} %t_hbm.1, f32[4096,8192]{1,0:T(8,128)} %v_hbm.1, f32[128,16384]{1,0:T(8,128)} %bitcast.3), custom_call_target="tpu_custom_call" | custom-call | tf_op jit(solution)/shard_map/back_transform/pallas_call | solution.py:474
  1126.6 8.9 copy.5

commit v3 on v2

--- a/solution.py
+++ b/solution.py
@@ -37,17 +37,18 @@
     return p[0:m] + (p[m:2 * m] + q[0:m]) + (p[2 * m:] + q[m:] + r)
 
 
-def kernel(R, NB, t_hbm, v_hbm, z_hbm, out_hbm,
-           xT, vst, vb, tst, tp, ysp, xsa, xsb, wacc, wsend, wrecv, ysend, yT,
+def kernel(H, NB, t_hbm, v_hbm, z_hbm, out_hbm,
+           xT, vst, vb, tst, tp, ysp, xs, wacc, wsend, wrecv, ysend, yT,
            gacc, gsend, grecv, gown, gfull, t01s, t01r,
            z_send, z_recv, z_loc, v_send, v_recv, v_loc, t_send, t_recv, t_loc,
            rs_send, rs_recv, ag_send, ag_recv, g_sems, p_send, p_recv, o_sem, vfree):
     NL = xT.shape[1]
-    NTL = NL // R
-    TB = R // 64
-    H = R // 2
-    G = R // 4
-    ZP = R // 128
+    M = NL // H
+    TB = H // 64
+    K = H // 2
+    S = H // 8
+    ZP = H // 128
+    FLAT = M - 5
     me = lax.axis_index('row')
     e = lax.axis_index('col')
     px, py = lax.rem(me, 2), me // 2
@@ -55,7 +56,7 @@
     mine = pl.ds(pl.multiple_of(me * SH, SH), SH)
 
     def rows_of(t):
-        return pl.ds(pl.multiple_of(t * R, R), R)
+        return pl.ds(pl.multiple_of(t * H, H), H)
 
     def chunk(c):
         return pl.ds(pl.multiple_of(c * C, C), C)
@@ -135,7 +136,7 @@
         def one(t, _):
             fn(q, t)
             return 0
-        lax.fori_loop(lo_v(q), NTL, one, 0)
+        lax.fori_loop(lo_v(q), M, one, 0)
 
     def fetch(q):
         def one(q, t):
@@ -163,16 +164,18 @@
         pl.semaphore_wait(vfree, 1)
         fetch(q - 2)
 
-    def prep(q, r0, gram):
+    def prep(q, r0, n):
         s, s4 = lax.rem(q, 2), lax.rem(q, 4)
-        rows = pl.ds(pl.multiple_of(r0, G), G)
-        f0, f1 = vst[s, 0, rows, :], vst[s, 1, rows, :]
-        p0, p1 = split3(f0), split3(f1)
-        for k in range(3):
-            vb[s4, k, rows, 0:128] = p0[k]
-            vb[s4, k, rows, 128:256] = p1[k]
-        if gram:
-            gacc[...] += dot6(128, jnp.concatenate(split3(f0.T), axis=0), *p1)
+        rows = pl.ds(pl.multiple_of(r0, 16), n)
+        for h in range(2):
+            for k, piece in enumerate(split3(vst[s, h, rows, :])):
+                vb[s4, k, rows, h * 128:(h + 1) * 128] = piece
+
+    def add_gram(q, r0, n):
+        s = lax.rem(q, 2)
+        rows = pl.ds(pl.multiple_of(r0, 16), n)
+        v0t = jnp.concatenate(split3(vst[s, 0, rows, :].T), axis=0)
+        gacc[...] += dot6(128, v0t, *split3(vst[s, 1, rows, :]))
 
     def g_start(q):
         gsend[...] = gacc[...]
@@ -219,33 +222,44 @@
             t01_copy(q).wait_recv()
             put(t01r[sh])
 
-    def upd(b, c, r0, xs):
+    def upd(b, c, r0, j, n=K):
         s4 = lax.rem(b, 4)
-        rows = pl.ds(pl.multiple_of(r0, H), H)
-        d = dot6(C, ysp[...], vb[s4, 0, rows, :], vb[s4, 1, rows, :], vb[s4, 2, rows, :], NT)
-        x = xT[chunk(c), rows] - d
+        rows = pl.ds(pl.multiple_of(r0, n), n)
+        x = xT[chunk(c), rows] - dot6(C, ysp[...], vb[s4, 0, rows, :], vb[s4, 1, rows, :], vb[s4, 2, rows, :], NT)
         xT[chunk(c), rows] = x
-        if xs is not None:
+        if j is not None:
             for i, piece in enumerate(split3(x)):
-                xs[i * C:(i + 1) * C, :] = piece
-
-    def wprod(q, r0, xs):
+                xs[j, i * C:(i + 1) * C, :] = piece
+
+    def wprod(q, r0, j):
         s4 = lax.rem(q, 4)
-        rows = pl.ds(pl.multiple_of(r0, H), H)
-        return dot6(C, xs[...], vb[s4, 0, rows, :], vb[s4, 1, rows, :], vb[s4, 2, rows, :])
-
-    def body(b, c, t, first, gram):
-        lo = (b - 1) // TB
-        q = jnp.maximum(b - 3, 0)
-        ra = t * R
-        upd(b, c, ra, xsa)
-        prep(q, lo * R + (c * (NTL - lo) + (t - lo)) * G, gram)
-        w = None if first else wprod(b - 1, ra - H, xsb)
-        upd(b, c, ra + H, xsb)
-        if first:
-            wacc[...] = wprod(b - 1, ra, xsa)
-        else:
-            wacc[...] += w + wprod(b - 1, ra, xsa)
+        rows = pl.ds(pl.multiple_of(r0, K), K)
+        return dot6(C, xs[j], vb[s4, 0, rows, :], vb[s4, 1, rows, :], vb[s4, 2, rows, :])
+
+    def body(b, c, r0, v0, units, gram, first, pend):
+        q3 = jnp.maximum(b - 3, 0)
+        slots = [0, 1, 2, 3][4 - units:]
+        tail = []
+        for s in range(units):
+            back = s - 2
+            if back < 0 and pend is not None:
+                tail.append(wprod(pend[0], NL + back * K, 4 + back))
+                if len(tail) == 2:
+                    wsend[pend[1]] = (wacc[0] + tail[0]) + (wacc[1] + tail[1])
+            elif back < 0 and not first:
+                wacc[s % 2] += wprod(b - 1, r0 + back * K, 4 + back)
+            upd(b, c, r0 + s * K, slots[s])
+            if back >= 0:
+                d = wprod(b - 1, r0 + back * K, slots[back])
+                if first:
+                    wacc[s % 2] = d
+                else:
+                    wacc[s % 2] += d
+            prep(q3, v0 + s * S, S)
+        if gram:
+            add_gram(q3, v0, units * S)
+        if first and units == 2:
+            wacc[...] = jnp.zeros_like(wacc)
 
     def rs_wait(j):
         for p in range(3):
@@ -298,19 +312,20 @@
     fetch(NB - 2)
 
     def z_first(n, _):
-        z_start(NTL * ZP - 1 - n)
+        z_start(M * ZP - 1 - n)
         return 0
     lax.fori_loop(0, ZP, z_first, 0)
 
     def prep_all(q):
         arrived(q)
 
-        def one(n, _):
-            prep(q, lo_v(q) * R + n * G, True)
+        def one(t, _):
+            add_gram(q, t * H, H)
+            prep(q, t * H, H)
             return 0
 
         gacc[...] = jnp.zeros_like(gacc)
-        lax.fori_loop(0, 4 * (NTL - lo_v(q)), one, 0)
+        lax.fori_loop(lo_v(q), M, one, 0)
 
     def when_own(q, fn):
         @pl.when(own(q))
@@ -331,14 +346,13 @@
     when_own(NB - 3, g_start)
     t_build(NB - 1)
     release(NB - 3)
-    z_wait(NTL - 1)
+    z_wait(M - 1)
 
     def first_w(c, _):
-        base = (NTL - 1) * R
-        for n, xs in enumerate((xsa, xsb)):
-            for i, piece in enumerate(split3(xT[chunk(c), base + n * H:base + (n + 1) * H])):
-                xs[i * C:(i + 1) * C, :] = piece
-        wsend[c] = wprod(NB - 1, base, xsa) + wprod(NB - 1, base + H, xsb)
+        for n in range(2):
+            for i, piece in enumerate(split3(xT[chunk(c), NL - (2 - n) * K:NL - (1 - n) * K])):
+                xs[2 + n, i * C:(i + 1) * C, :] = piece
+        wsend[c] = wprod(NB - 1, NL - 2 * K, 2) + wprod(NB - 1, NL - K, 3)
         w_send(c)
         return 0
     lax.fori_loop(0, 4, first_w, 0)
@@ -347,6 +361,8 @@
         rs_sum(j)
         y_send(j)
 
+    FIRST = TB * (FLAT + 1)
+
     def slot(i, _):
         b = NB - 1 - i // 4
         c = lax.rem(i, 4)
@@ -359,9 +375,11 @@
             def _():
                 z_wait(lo)
 
-            @pl.when(jnp.logical_and(lo >= 1, lax.rem(TB * (lo + 1) - 1 - b, TB // ZP) == 0))
-            def _():
-                z_start((lo - 1) * ZP + ZP - 1 - (TB * (lo + 1) - 1 - b) // (TB // ZP))
+            back = TB * (lo + 1) - 1 - b
+
+            @pl.when(jnp.logical_and(jnp.logical_and(lo >= 1, back >= 0), lax.rem(back, TB // ZP) == 0))
+            def _():
+                z_start(lo * ZP - 1 - back // (TB // ZP))
 
             @pl.when(q3 >= 0)
             def _():
@@ -375,40 +393,70 @@
                 g_mid(b - 2)
             t_build(b - 1)
 
-        @pl.when(jnp.logical_and(q3 >= 0, lo_v(q3) < lo))
-        def _():
-            @pl.when(own(q3))
-            def _():
-                prep(q3, lo_v(q3) * R + c * G, True)
-
-            @pl.when(jnp.logical_not(own(q3)))
-            def _():
-                prep(q3, lo_v(q3) * R + c * G, False)
-
-        def run(gram):
-            y_take(c)
-            body(b, c, lo, True, gram)
-
-            def tile(t, _):
-                body(b, c, t, False, gram)
+        with_gram = jnp.logical_and(q3 >= 0, own(q3))
+        m = M - lo
+        odd = lax.rem(m, 2)
+        flat = lo <= FLAT
+        base = lo * H
+        v0 = base + c * (m * 2 * S)
+
+        def above(t, _):
+            r0 = t * H + c * (2 * S)
+
+            @pl.when(with_gram)
+            def _():
+                add_gram(q3, r0, 2 * S)
+            prep(q3, r0, 2 * S)
+            return 0
+        lax.fori_loop(jnp.where(q3 >= 0, lo_v(q3), lo), lo, above, 0)
+
+        y_take(c)
+
+        def first_body(gram, pend):
+            for units in (2, 4):
+                @pl.when(odd == (units == 2))
+                def _():
+                    body(b, c, base, v0, units, gram, True, pend)
+
+        def more(gram, start, stop):
+            def tile(k, _):
+                body(b, c, base + (2 - odd) * H + k * (2 * H), v0 + ((2 - odd) * 2 + 4 * k) * S, 4, gram, False, None)
                 return 0
-            lax.fori_loop(lo + 1, NTL, tile, 0)
-
-        with_gram = jnp.logical_and(q3 >= 0, own(q3))
-
-        @pl.when(with_gram)
-        def _():
-            run(True)
-
-        @pl.when(jnp.logical_not(with_gram))
-        def _():
-            run(False)
-
-        rs_wait(i + 2)
-        rs_sum(i + 2)
-        wsend[c] = wacc[...] + wprod(b - 1, NL - H, xsb)
-        y_send(i + 2)
-        w_send(c)
+            lax.fori_loop(start, stop, tile, 0)
+
+        whole = (m + odd) // 2 - 1
+
+        for gram in (True, False):
+            @pl.when(jnp.logical_and(jnp.logical_not(flat), with_gram == gram))
+            def _():
+                first_body(gram, None)
+                more(gram, 0, whole)
+
+        @pl.when(jnp.logical_not(flat))
+        def _():
+            rs_wait(i + 2)
+            rs_sum(i + 2)
+            wsend[c] = (wacc[0] + wprod(b - 1, NL - 2 * K, 2)) + (wacc[1] + wprod(b - 1, NL - K, 3))
+            y_send(i + 2)
+            w_send(c)
+
+        before = lax.rem(c + 3, 4)
+        begin = jnp.logical_and(b == FIRST, c == 0)
+        pend = (jnp.where(c == 0, b, b - 1), jnp.where(begin, 4, before))
+
+        for gram in (True, False):
+            @pl.when(jnp.logical_and(flat, with_gram == gram))
+            def _():
+                first_body(gram, pend)
+
+                @pl.when(jnp.logical_not(begin))
+                def _():
+                    w_send(before)
+                more(gram, 0, 1)
+                rs_wait(i + 2)
+                rs_sum(i + 2)
+                y_send(i + 2)
+                more(gram, 1, whole)
 
         @pl.when(c == 3)
         def _():
@@ -426,6 +474,8 @@
         return 0
 
     lax.fori_loop(0, 4 * (NB - 1), slot, 0)
+    wsend[3] = (wacc[0] + wprod(0, NL - 2 * K, 2)) + (wacc[1] + wprod(0, NL - K, 3))
+    w_send(3)
 
     def out_copy(c):
         return pltpu.make_async_copy(xT.at[chunk(c), :], out_hbm.at[chunk(c), :], o_sem.at[c])
@@ -440,10 +490,9 @@
         y_take(c)
 
         def tile(t, _):
-            upd(0, c, t * R, None)
-            upd(0, c, t * R + H, None)
+            upd(0, c, t * 2 * H, None, 2 * H)
             return 0
-        lax.fori_loop(0, NTL, tile, 0)
+        lax.fori_loop(0, M // 2, tile, 0)
         out_copy(c).start()
         return 0
     lax.fori_loop(0, 4, end_slot, 0)
@@ -455,7 +504,7 @@
         for p in range(3):
             z_remote(k, p).wait_send()
         return 0
-    lax.fori_loop(0, NTL * ZP, z_sent, 0)
+    lax.fori_loop(0, M * ZP, z_sent, 0)
     sent(1)
     sent(0)
 
@@ -464,15 +513,14 @@
     def local_apply(v_loc, t_loc, z_loc):
         NL, half = v_loc.shape
         NB = half // 128
-        R = min(1024, NL // 2)
-        tiles = NL // R
-        H = R // 2
+        H = min(512, NL // 8)
+        tiles = NL // H
         z_t = z_loc.T
         any_ = pl.BlockSpec(memory_space=pl.ANY)
         dma = pltpu.SemaphoreType.DMA
         vmem = pltpu.VMEM
         x_t = pl.pallas_call(
-            functools.partial(kernel, R, NB),
+            functools.partial(kernel, H, NB),
             out_shape=jax.ShapeDtypeStruct((4 * C, NL), F32),
             in_specs=[any_] * 3,
             out_specs=any_,
@@ -483,10 +531,9 @@
                 vmem((4, 2, 128, 128), F32),
                 vmem((2, 3, B, B), BF16),
                 vmem((3 * C, B), BF16),
-                vmem((3 * C, H), BF16),
-                vmem((3 * C, H), BF16),
-                vmem((C, B), F32),
-                vmem((4, C, B), F32),
+                vmem((4, 3 * C, H // 2), BF16),
+                vmem((2, C, B), F32),
+                vmem((5, C, B), F32),
                 vmem((4, 3, SH, B), F32),
                 vmem((4, SH, B), F32),
                 vmem((4, C, B), F32),

time: 1140 us -> 1090 us (0.956)
  Pallas kernels: 1120 us -> 1070 us
    pallas_call x1, Pallas kernels: 1120 us -> 1070 us  [local_apply(): pl.pallas_call(functools.partial(kernel, H, NB), out_shape=jax.ShapeDtype...]
where the time goes in v3:
time: 1090 us
  Pallas kernels  1070 us (98%)
  local copies, waits for them, and re-layouts  17.9 us (2%)
    pallas_call x1, Pallas kernels, local_apply(): pl.pallas_call(functools.partial(kernel, H, NB), out_shape=jax.ShapeDtype...  1070 us

profile of v3, /device:TPU:0, one launch (start us, length us, event | category | flops | bytes accessed | tf_op | source)
XLA Modules:
  0.0 1085.5 jit_solution(613910499990255890)
XLA Ops:
  0.0 9.0 copy.4
  9.0 1067.5 %back_transform.1 = f32[512,4096]{1,0:T(8,128)} custom-call(f32[64,128,128]{2,1,0:T(8,128)} %t_hbm.1, f32[4096,8192]{1,0:T(8,128)} %v_hbm.1, f32[128,16384]{1,0:T(8,128)} %bitcast.3), custom_call_target="tpu_custom_call" | custom-call | tf_op jit(solution)/shard_map/back_transform/pallas_call | solution.py:522
  1076.5 8.9 copy.5

commit v4 on v3

--- a/solution.py
+++ b/solution.py
@@ -7,7 +7,6 @@
 from jax.experimental.pallas import tpu as pltpu
 from jax.sharding import PartitionSpec as P
 
-HIGHEST = lax.Precision.HIGHEST
 F32 = jnp.float32
 BF16 = jnp.bfloat16
 MESH = pl.DeviceIdType.MESH
@@ -16,6 +15,16 @@
 C = 128
 B = 256
 SH = 32
+CORES, CHIPS3, CHIPS4 = range(2), range(3), range(4)
+FLAT_FROM = 5
+TAIL = 4
+
+
+def loop(start, stop, fn):
+    def step(i, carry):
+        fn(i)
+        return carry
+    lax.fori_loop(start, stop, step, 0)
 
 
 def dg(a, b, dims=NN):
@@ -39,16 +48,19 @@
 
 def kernel(H, NB, t_hbm, v_hbm, z_hbm, out_hbm,
            xT, vst, vb, tst, tp, ysp, xs, wacc, wsend, wrecv, ysend, yT,
-           gacc, gsend, grecv, gown, gfull, t01s, t01r,
+           gacc, gsend, grecv, gown, gfull, t01s, t01r, vtail, ttail, xtail,
            z_send, z_recv, z_loc, v_send, v_recv, v_loc, t_send, t_recv, t_loc,
-           rs_send, rs_recv, ag_send, ag_recv, g_sems, p_send, p_recv, o_sem, vfree):
+           rs_send, rs_recv, ag_send, ag_recv, g_sems, p_send, p_recv, o_sem, e_sems, d_sems, l_sem, x_sems, vfree):
     NL = xT.shape[1]
     M = NL // H
     TB = H // 64
     K = H // 2
     S = H // 8
     ZP = H // 128
-    FLAT = M - 5
+    B0 = NB - 1 - TAIL
+    RT = 64 * TAIL
+    ZE = (NL - RT) // 128
+    FLAT = FLAT_FROM
     me = lax.axis_index('row')
     e = lax.axis_index('col')
     px, py = lax.rem(me, 2), me // 2
@@ -132,11 +144,58 @@
             src_ref=gown, dst_ref=gfull.at[mine, :], send_sem=g_sems.at[2, p], recv_sem=g_sems.at[3, p],
             device_id=(peers[p], e), device_id_type=MESH)
 
+    def top(k):
+        return 64 * k // 128 * 128
+
+    def e_remote(k, p):
+        n = RT - top(k)
+        return pltpu.make_async_remote_copy(
+            src_ref=v_hbm.at[NL - n:, (B0 + 1 + k) * 128:(B0 + 2 + k) * 128],
+            dst_ref=vtail.at[k, e, me, RT - n:, :],
+            send_sem=e_sems.at[0, k, p], recv_sem=e_sems.at[1, k, p],
+            device_id=(peers[p], e), device_id_type=MESH)
+
+    def e_local(k):
+        n = RT - top(k)
+        return pltpu.make_async_copy(
+            v_hbm.at[NL - n:, (B0 + 1 + k) * 128:(B0 + 2 + k) * 128],
+            vtail.at[k, e, me, RT - n:, :], l_sem.at[0, k])
+
+    def d_remote(k, p):
+        n = RT - top(k)
+        if p == 3:
+            src, chip = v_hbm.at[NL - n:, (B0 + 1 + k) * 128:(B0 + 2 + k) * 128], me
+        else:
+            chip = peers[p]
+            src = vtail.at[k, e, chip, RT - n:, :]
+        return pltpu.make_async_remote_copy(
+            src_ref=src, dst_ref=vtail.at[k, e, chip, RT - n:, :],
+            send_sem=d_sems.at[0, k, p], recv_sem=d_sems.at[1, k, p],
+            device_id=(me, 1 - e), device_id_type=MESH)
+
+    def f_remote(k):
+        return pltpu.make_async_remote_copy(
+            src_ref=t_hbm.at[B0 + 1 + k], dst_ref=ttail.at[k, e],
+            send_sem=d_sems.at[0, k, 4], recv_sem=d_sems.at[1, k, 4],
+            device_id=(me, 1 - e), device_id_type=MESH)
+
+    def f_local(k):
+        return pltpu.make_async_copy(t_hbm.at[B0 + 1 + k], ttail.at[k, e], l_sem.at[1, k])
+
+    def h_local(d):
+        return pltpu.make_async_copy(z_hbm.at[:, (d + 1) * NL - RT:(d + 1) * NL], xtail.at[:, d * RT:(d + 1) * RT],
+                                     l_sem.at[2, d])
+
+    def x_remote(p):
+        return pltpu.make_async_remote_copy(
+            src_ref=xtail.at[:, pl.ds(pl.multiple_of(peers[p] * RT, RT), RT)],
+            dst_ref=xT.at[chunk(me), NL - RT:], send_sem=x_sems.at[0, p], recv_sem=x_sems.at[1, p],
+            device_id=(peers[p], e), device_id_type=MESH)
+
     def over_tiles(q, fn):
-        def one(t, _):
+        def one(t):
             fn(q, t)
-            return 0
-        lax.fori_loop(lo_v(q), M, one, 0)
+        loop(lo_v(q), M, one)
 
     def fetch(q):
         def one(q, t):
@@ -167,7 +226,7 @@
     def prep(q, r0, n):
         s, s4 = lax.rem(q, 2), lax.rem(q, 4)
         rows = pl.ds(pl.multiple_of(r0, 16), n)
-        for h in range(2):
+        for h in CORES:
             for k, piece in enumerate(split3(vst[s, h, rows, :])):
                 vb[s4, k, rows, h * 128:(h + 1) * 128] = piece
 
@@ -179,48 +238,51 @@
 
     def g_start(q):
         gsend[...] = gacc[...]
-        for p in range(3):
+        for p in CHIPS3:
             grs_copy(p).start()
 
     def g_mid(q):
-        for p in range(3):
+        for p in CHIPS3:
             grs_copy(p).wait_recv()
         g = (gsend[mine, :] + grecv[0]) + (grecv[1] + grecv[2])
         gown[...] = g
         gfull[mine, :] = g
-        for p in range(3):
+        for p in CHIPS3:
             gag_copy(p).start()
 
     def g_fin(q):
-        for p in range(3):
+        for p in CHIPS3:
             gag_copy(p).wait_recv()
             grs_copy(p).wait_send()
             gag_copy(p).wait_send()
         s = lax.rem(q, 4)
-        u = lax.dot_general(tst[s, 0], gfull[...], NN, precision=HIGHEST, preferred_element_type=F32)
-        t01 = -lax.dot_general(u, tst[s, 1], NN, precision=HIGHEST, preferred_element_type=F32)
+        t01 = t_cross(tst[s, 0], gfull[...], tst[s, 1])
         t01s[lax.rem(q // 2, 2)] = t01
         t01_copy(q).start()
 
+    def t_put(s2, t0, t1, t01):
+        tt = jnp.concatenate([
+            jnp.concatenate([t0.T, jnp.zeros((128, 128), F32)], axis=1),
+            jnp.concatenate([t01.T, t1.T], axis=1)], axis=0)
+        for k, piece in enumerate(split3(tt)):
+            tp[s2, k] = piece
+
+    def t_cross(t0, g, t1):
+        u = dot6(128, jnp.concatenate(split3(t0), axis=0), *split3(g))
+        return -dot6(128, jnp.concatenate(split3(u), axis=0), *split3(t1))
+
     def t_build(q):
         s, s2, sh = lax.rem(q, 4), lax.rem(q, 2), lax.rem(q // 2, 2)
-
-        def put(t01):
-            tt = jnp.concatenate([
-                jnp.concatenate([tst[s, 0].T, jnp.zeros((128, 128), F32)], axis=1),
-                jnp.concatenate([t01.T, tst[s, 1].T], axis=1)], axis=0)
-            for k, piece in enumerate(split3(tt)):
-                tp[s2, k] = piece
 
         @pl.when(own(q))
         def _():
             t01_copy(q).wait_send()
-            put(t01s[sh])
+            t_put(s2, tst[s, 0], tst[s, 1], t01s[sh])
 
         @pl.when(jnp.logical_not(own(q)))
         def _():
             t01_copy(q).wait_recv()
-            put(t01r[sh])
+            t_put(s2, tst[s, 0], tst[s, 1], t01r[sh])
 
     def upd(b, c, r0, j, n=K):
         s4 = lax.rem(b, 4)
@@ -236,17 +298,12 @@
         rows = pl.ds(pl.multiple_of(r0, K), K)
         return dot6(C, xs[j], vb[s4, 0, rows, :], vb[s4, 1, rows, :], vb[s4, 2, rows, :])
 
-    def body(b, c, r0, v0, units, gram, first, pend):
+    def body(b, c, r0, v0, units, gram, first):
         q3 = jnp.maximum(b - 3, 0)
         slots = [0, 1, 2, 3][4 - units:]
-        tail = []
         for s in range(units):
             back = s - 2
-            if back < 0 and pend is not None:
-                tail.append(wprod(pend[0], NL + back * K, 4 + back))
-                if len(tail) == 2:
-                    wsend[pend[1]] = (wacc[0] + tail[0]) + (wacc[1] + tail[1])
-            elif back < 0 and not first:
+            if back < 0 and not first:
                 wacc[s % 2] += wprod(b - 1, r0 + back * K, 4 + back)
             upd(b, c, r0 + s * K, slots[s])
             if back >= 0:
@@ -261,28 +318,52 @@
         if first and units == 2:
             wacc[...] = jnp.zeros_like(wacc)
 
+    def half(b, c, m, v0, second, pend, gram):
+        q3 = jnp.maximum(b - 3, 0)
+        base = NL - m * H
+        cut = m // 2 * 2
+        for s in range(cut, 2 * m) if second else range(cut):
+            back = s - 2
+            if back < 0:
+                d = wprod(pend[0], NL + back * K, 4 + back)
+                if back == -2:
+                    held = d
+                else:
+                    wsend[pend[1]] = (wacc[0] + held) + (wacc[1] + d)
+            upd(b, c, base + s * K, (s - 2 * m) % 4)
+            if back >= 0:
+                d = wprod(b - 1, base + back * K, (back - 2 * m) % 4)
+                if back < 2:
+                    wacc[back] = d
+                else:
+                    wacc[back % 2] += d
+            prep(q3, v0 + s * S, S)
+        if gram:
+            for n in range(0, 2 * m, 4):
+                add_gram(q3, v0 + n * S, min(4, 2 * m - n) * S)
+
     def rs_wait(j):
-        for p in range(3):
+        for p in CHIPS3:
             rs_copy(lax.rem(j, 4), p).wait_recv()
 
     def rs_sum(j):
         c = lax.rem(j, 4)
-        s2 = lax.rem(NB - 1 - j // 4, 2)
+        s2 = lax.rem(B0 - j // 4, 2)
         w = (wsend[c, mine, :] + wrecv[c, 0]) + (wrecv[c, 1] + wrecv[c, 2])
         y = dot6(SH, jnp.concatenate(split3(w), axis=0), tp[s2, 0], tp[s2, 1], tp[s2, 2])
         ysend[c] = y
         yT[c, mine, :] = y
 
     def y_send(j):
-        for p in range(3):
+        for p in CHIPS3:
             ag_copy(lax.rem(j, 4), p).start()
 
     def w_send(c):
-        for p in range(3):
+        for p in CHIPS3:
             rs_copy(c, p).start()
 
     def y_take(c):
-        for p in range(3):
+        for p in CHIPS3:
             ag_copy(c, p).wait_recv()
             ag_copy(c, p).wait_send()
             rs_copy(c, p).wait_send()
@@ -290,81 +371,152 @@
             ysp[i * C:(i + 1) * C, :] = piece
 
     def z_start(k):
-        for p in range(3):
+        for p in CHIPS3:
             z_remote(k, p).start()
         z_local(k).start()
 
     def z_wait(t):
-        def one(k, _):
+        def one(k):
             z_local(k).wait()
-            for p in range(3):
+            for p in CHIPS3:
                 z_remote(k, p).wait_recv()
-            return 0
-        lax.fori_loop(t * ZP, (t + 1) * ZP, one, 0)
+        loop(t * ZP, (t + 1) * ZP, one)
 
     barrier = pltpu.get_barrier_semaphore()
-    for p in range(3):
+    for p in CHIPS3:
         pl.semaphore_signal(barrier, inc=1, device_id=(peers[p], e), device_id_type=MESH)
     pl.semaphore_signal(barrier, inc=1, device_id=(me, 1 - e), device_id_type=MESH)
     pl.semaphore_wait(barrier, 4)
 
-    fetch(NB - 1)
-    fetch(NB - 2)
-
-    def z_first(n, _):
-        z_start(M * ZP - 1 - n)
-        return 0
-    lax.fori_loop(0, ZP, z_first, 0)
+    for k in reversed(range(TAIL)):
+        for p in CHIPS3:
+            e_remote(k, p).start()
+        e_local(k).start()
+        d_remote(k, 3).start()
+        f_remote(k).start()
+        f_local(k).start()
+    for d in CHIPS4:
+        h_local(d).start()
+    fetch(B0)
+    fetch(B0 - 1)
+
+    def z_first(n):
+        z_start(ZE - 1 - n)
+    ZS = (B0 - 1) // TB * ZP
+    late = TB - 1 - (B0 - 1) % TB - 1
+    step = TB // ZP
+    loop(0, ZE - ZS + (late + step - 1) // step, z_first)
 
     def prep_all(q):
         arrived(q)
 
-        def one(t, _):
+        def one(t):
             add_gram(q, t * H, H)
             prep(q, t * H, H)
-            return 0
 
         gacc[...] = jnp.zeros_like(gacc)
-        lax.fori_loop(lo_v(q), M, one, 0)
+        loop(lo_v(q), M, one)
 
     def when_own(q, fn):
         @pl.when(own(q))
         def _():
             fn(q)
 
-    prep_all(NB - 1)
-    when_own(NB - 1, g_start)
-    release(NB - 1)
-    prep_all(NB - 2)
-    when_own(NB - 2, g_start)
-    release(NB - 2)
-    when_own(NB - 1, g_mid)
-    when_own(NB - 2, g_mid)
-    when_own(NB - 1, g_fin)
-    when_own(NB - 2, g_fin)
-    prep_all(NB - 3)
-    when_own(NB - 3, g_start)
-    t_build(NB - 1)
-    release(NB - 3)
-    z_wait(M - 1)
-
-    def first_w(c, _):
-        for n in range(2):
-            for i, piece in enumerate(split3(xT[chunk(c), NL - (2 - n) * K:NL - (1 - n) * K])):
-                xs[2 + n, i * C:(i + 1) * C, :] = piece
-        wsend[c] = wprod(NB - 1, NL - 2 * K, 2) + wprod(NB - 1, NL - K, 3)
+    def corner_pass(k):
+        for p in CHIPS3:
+            e_remote(k, p).wait_recv()
+            d_remote(k, p).start()
+
+    def corner(k):
+        o = top(k)
+        n = RT - o
+        free = (B0 + 1) % 4
+        e_local(k).wait()
+        f_local(k).wait()
+        f_remote(k).wait_recv()
+        for p in CHIPS4:
+            d_remote(k, p).wait_recv()
+        gacc[...] = jnp.zeros_like(gacc)
+
+        def split_chip(d):
+            rows = pl.ds(pl.multiple_of(d * n, 128), n)
+            f0, f1 = vtail[k, 0, d, o:, :], vtail[k, 1, d, o:, :]
+            p0, p1 = split3(f0), split3(f1)
+            for j in CHIPS3:
+                vb[free, j, rows, 0:128] = p0[j]
+                vb[free, j, rows, 128:256] = p1[j]
+            gacc[...] += dot6(128, jnp.concatenate(split3(f0.T), axis=0), *p1)
+        loop(0, 4, split_chip)
+        t_put(0, ttail[k, 0], ttail[k, 1], t_cross(ttail[k, 0], gacc[...], ttail[k, 1]))
+        w = None
+        for d in CHIPS4:
+            x = jnp.concatenate(split3(xtail[:, d * RT + o:(d + 1) * RT]), axis=0)
+            r = slice(d * n, (d + 1) * n)
+            part = dot6(C, x, vb[free, 0, r, :], vb[free, 1, r, :], vb[free, 2, r, :])
+            w = part if w is None else w + part
+        y = dot6(C, jnp.concatenate(split3(w), axis=0), tp[0, 0], tp[0, 1], tp[0, 2])
+        for i, piece in enumerate(split3(y)):
+            ysp[i * C:(i + 1) * C, :] = piece
+        for d in CHIPS4:
+            r = slice(d * n, (d + 1) * n)
+            xtail[:, d * RT + o:(d + 1) * RT] -= dot6(
+                C, ysp[...], vb[free, 0, r, :], vb[free, 1, r, :], vb[free, 2, r, :], NT)
+
+    prep_all(B0)
+    when_own(B0, g_start)
+    release(B0)
+    prep_all(B0 - 1)
+    when_own(B0 - 1, g_start)
+    release(B0 - 1)
+    for d in CHIPS4:
+        h_local(d).wait()
+    corner_pass(TAIL - 1)
+    for k in reversed(range(TAIL)):
+        if k:
+            corner_pass(k - 1)
+        corner(k)
+    for p in CHIPS3:
+        x_remote(p).start()
+    xT[chunk(me), NL - RT:] = xtail[:, pl.ds(pl.multiple_of(me * RT, RT), RT)]
+    when_own(B0, g_mid)
+    when_own(B0 - 1, g_mid)
+    when_own(B0, g_fin)
+    when_own(B0 - 1, g_fin)
+    prep_all(B0 - 2)
+    when_own(B0 - 2, g_start)
+    t_build(B0)
+    release(B0 - 2)
+
+    def z_first_wait(k):
+        z_local(k).wait()
+        for p in CHIPS3:
+            z_remote(k, p).wait_recv()
+    loop(ZS, ZE, z_first_wait)
+    for p in CHIPS3:
+        x_remote(p).wait_recv()
+
+    def first_w(c):
+        wacc[...] = jnp.zeros_like(wacc)
+
+        def one(t):
+            for n in CORES:
+                r0 = t * H + n * K
+                for i, piece in enumerate(split3(xT[chunk(c), pl.ds(pl.multiple_of(r0, K), K)])):
+                    xs[2 + n, i * C:(i + 1) * C, :] = piece
+                wacc[n] += wprod(B0, r0, 2 + n)
+        loop(B0 // TB, M, one)
+        wsend[c] = wacc[0] + wacc[1]
         w_send(c)
-        return 0
-    lax.fori_loop(0, 4, first_w, 0)
-    for j in range(2):
+    loop(0, 4, first_w)
+    for j in CORES:
         rs_wait(j)
         rs_sum(j)
         y_send(j)
 
-    FIRST = TB * (FLAT + 1)
-
-    def slot(i, _):
-        b = NB - 1 - i // 4
+    FIRST = TB * (M - FLAT + 1)
+
+    def slot(i):
+        b = B0 - i // 4
         c = lax.rem(i, 4)
         lo = (b - 1) // TB
         q3 = b - 3
@@ -395,68 +547,62 @@
 
         with_gram = jnp.logical_and(q3 >= 0, own(q3))
         m = M - lo
-        odd = lax.rem(m, 2)
-        flat = lo <= FLAT
         base = lo * H
         v0 = base + c * (m * 2 * S)
 
-        def above(t, _):
+        def above(t):
             r0 = t * H + c * (2 * S)
 
             @pl.when(with_gram)
             def _():
                 add_gram(q3, r0, 2 * S)
             prep(q3, r0, 2 * S)
-            return 0
-        lax.fori_loop(jnp.where(q3 >= 0, lo_v(q3), lo), lo, above, 0)
-
-        y_take(c)
-
-        def first_body(gram, pend):
-            for units in (2, 4):
-                @pl.when(odd == (units == 2))
-                def _():
-                    body(b, c, base, v0, units, gram, True, pend)
-
-        def more(gram, start, stop):
-            def tile(k, _):
-                body(b, c, base + (2 - odd) * H + k * (2 * H), v0 + ((2 - odd) * 2 + 4 * k) * S, 4, gram, False, None)
-                return 0
-            lax.fori_loop(start, stop, tile, 0)
-
-        whole = (m + odd) // 2 - 1
-
-        for gram in (True, False):
-            @pl.when(jnp.logical_and(jnp.logical_not(flat), with_gram == gram))
-            def _():
-                first_body(gram, None)
-                more(gram, 0, whole)
-
-        @pl.when(jnp.logical_not(flat))
-        def _():
-            rs_wait(i + 2)
-            rs_sum(i + 2)
-            wsend[c] = (wacc[0] + wprod(b - 1, NL - 2 * K, 2)) + (wacc[1] + wprod(b - 1, NL - K, 3))
-            y_send(i + 2)
-            w_send(c)
+        loop(jnp.where(q3 >= 0, lo_v(q3), lo), lo, above)
 
         before = lax.rem(c + 3, 4)
         begin = jnp.logical_and(b == FIRST, c == 0)
         pend = (jnp.where(c == 0, b, b - 1), jnp.where(begin, 4, before))
 
-        for gram in (True, False):
-            @pl.when(jnp.logical_and(flat, with_gram == gram))
-            def _():
-                first_body(gram, pend)
+        def start(m, gram):
+            @pl.when(with_gram == gram)
+            def _():
+                y_take(c)
+                if m >= FLAT:
+                    half(b, c, m, v0, False, pend, gram)
+                else:
+                    body(b, c, base, v0, 4 - m % 2 * 2, gram, True)
+
+        for odd in (0, 1):
+            @pl.when(jnp.logical_and(lo > M - FLAT, lax.rem(m, 2) == odd))
+            def _():
+                for gram in (True, False):
+                    start(odd, gram)
+
+                    @pl.when(with_gram == gram)
+                    def _():
+                        def tile(k):
+                            n = 2 - odd + 2 * k
+                            body(b, c, base + n * H, v0 + 2 * n * S, 4, gram, False)
+                        loop(0, (m + odd) // 2 - 1, tile)
+                rs_wait(i + 2)
+                rs_sum(i + 2)
+                wsend[c] = (wacc[0] + wprod(b - 1, NL - 2 * K, 2)) + (wacc[1] + wprod(b - 1, NL - K, 3))
+                y_send(i + 2)
+                w_send(c)
+
+        for tiles in range(FLAT, M + 1):
+            @pl.when(m == tiles)
+            def _():
+                for gram in (True, False):
+                    start(tiles, gram)
 
                 @pl.when(jnp.logical_not(begin))
                 def _():
                     w_send(before)
-                more(gram, 0, 1)
                 rs_wait(i + 2)
                 rs_sum(i + 2)
+                half(b, c, tiles, v0, True, None, False)
                 y_send(i + 2)
-                more(gram, 1, whole)
 
         @pl.when(c == 3)
         def _():
@@ -471,40 +617,45 @@
             @pl.when(q3 >= 2)
             def _():
                 release(q3)
-        return 0
-
-    lax.fori_loop(0, 4 * (NB - 1), slot, 0)
-    wsend[3] = (wacc[0] + wprod(0, NL - 2 * K, 2)) + (wacc[1] + wprod(0, NL - K, 3))
-    w_send(3)
+
+    loop(0, 4 * B0, slot)
+    if FLAT <= M:
+        wsend[3] = (wacc[0] + wprod(0, NL - 2 * K, 2)) + (wacc[1] + wprod(0, NL - K, 3))
+        w_send(3)
 
     def out_copy(c):
         return pltpu.make_async_copy(xT.at[chunk(c), :], out_hbm.at[chunk(c), :], o_sem.at[c])
 
-    def end_slot(c, _):
+    def end_slot(c):
         @pl.when(c < 2)
         def _():
-            j = 4 * (NB - 1) + c + 2
+            j = 4 * B0 + c + 2
             rs_wait(j)
             rs_sum(j)
             y_send(j)
         y_take(c)
 
-        def tile(t, _):
+        def tile(t):
             upd(0, c, t * 2 * H, None, 2 * H)
-            return 0
-        lax.fori_loop(0, M // 2, tile, 0)
+        loop(0, M // 2, tile)
         out_copy(c).start()
-        return 0
-    lax.fori_loop(0, 4, end_slot, 0)
+    loop(0, 4, end_slot)
 
     for c in range(4):
         out_copy(c).wait()
 
-    def z_sent(k, _):
-        for p in range(3):
+    def z_sent(k):
+        for p in CHIPS3:
             z_remote(k, p).wait_send()
-        return 0
-    lax.fori_loop(0, M * ZP, z_sent, 0)
+    loop(0, ZE, z_sent)
+    for p in CHIPS3:
+        x_remote(p).wait_send()
+        for k in range(TAIL):
+            e_remote(k, p).wait_send()
+    for k in range(TAIL):
+        f_remote(k).wait_send()
+        for p in CHIPS4:
+            d_remote(k, p).wait_send()
     sent(1)
     sent(0)
 
@@ -544,11 +695,13 @@
                 vmem((128, 128), F32),
                 vmem((2, 128, 128), F32),
                 vmem((2, 128, 128), F32),
+                vmem((TAIL, 2, 4, 64 * TAIL, 128), F32),
+                vmem((TAIL, 2, 128, 128), F32),
+                vmem((C, 4 * 64 * TAIL), F32),
                 dma((NL // 128, 3)), dma((NL // 128, 3)), dma((NL // 128,)),
-                dma((2, tiles)), dma((2, tiles)), dma((2, tiles)),
-                dma((4,)), dma((4,)), dma((4,)),
-                dma((4, 3)), dma((4, 3)), dma((4, 3)), dma((4, 3)),
-                dma((4, 3)), dma((2,)), dma((2,)), dma((4,)),
+                *[dma((2, tiles))] * 3, *[dma((4,))] * 3,
+                *[dma((4, 3))] * 5, dma((2,)), dma((2,)), dma((4,)),
+                dma((2, TAIL, 3)), dma((2, TAIL, 5)), dma((3, max(TAIL, 4))), dma((2, 3)),
                 pltpu.SemaphoreType.REGULAR,
             ],
             compiler_params=pltpu.CompilerParams(

time: 1090 us -> 1020 us (0.936)
  Pallas kernels: 1070 us -> 1000 us
    pallas_call x1, Pallas kernels: 1070 us -> 1000 us  [local_apply(): pl.pallas_call(functools.partial(kernel, H, NB), out_shape=jax.ShapeDtype...]
where the time goes in v4:
time: 1020 us
  Pallas kernels  1000 us (98%)
  local copies, waits for them, and re-layouts  17.9 us (2%)
    pallas_call x1, Pallas kernels, local_apply(): pl.pallas_call(functools.partial(kernel, H, NB), out_shape=jax.ShapeDtype...  1000 us

profile of v4, /device:TPU:0, one launch (start us, length us, event | category | flops | bytes accessed | tf_op | source)
XLA Modules:
  0.0 1019.1 jit_solution(4151239159288857630)
XLA Ops:
  0.0 9.0 copy.4
  9.0 1001.2 %back_transform.1 = f32[512,4096]{1,0:T(8,128)} custom-call(f32[64,128,128]{2,1,0:T(8,128)} %t_hbm.1, f32[4096,8192]{1,0:T(8,128)} %v_hbm.1, f32[128,16384]{1,0:T(8,128)} %bitcast.3), custom_call_target="tpu_custom_call" | custom-call | tf_op jit(solution)/shard_map/back_transform/pallas_call | solution.py:673
  1010.2 8.9 copy.5

commit v5 on v4

--- a/solution.py
+++ b/solution.py
@@ -17,7 +17,7 @@
 SH = 32
 CORES, CHIPS3, CHIPS4 = range(2), range(3), range(4)
 FLAT_FROM = 5
-TAIL = 4
+TAIL = 6
 
 
 def loop(start, stop, fn):
@@ -144,32 +144,23 @@
             src_ref=gown, dst_ref=gfull.at[mine, :], send_sem=g_sems.at[2, p], recv_sem=g_sems.at[3, p],
             device_id=(peers[p], e), device_id_type=MESH)
 
-    def top(k):
-        return 64 * k // 128 * 128
-
-    def e_remote(k, p):
-        n = RT - top(k)
-        return pltpu.make_async_remote_copy(
-            src_ref=v_hbm.at[NL - n:, (B0 + 1 + k) * 128:(B0 + 2 + k) * 128],
-            dst_ref=vtail.at[k, e, me, RT - n:, :],
+    def e_ref(k, g):
+        return v_hbm.at[NL - RT + g * 128:, pl.ds(pl.multiple_of((B0 + 1 + k) * 128, 128), 128)]
+
+    def e_remote(k, g, p):
+        return pltpu.make_async_remote_copy(
+            src_ref=e_ref(k, g), dst_ref=vtail.at[k, e, me, g * 128:, :],
             send_sem=e_sems.at[0, k, p], recv_sem=e_sems.at[1, k, p],
             device_id=(peers[p], e), device_id_type=MESH)
 
-    def e_local(k):
-        n = RT - top(k)
-        return pltpu.make_async_copy(
-            v_hbm.at[NL - n:, (B0 + 1 + k) * 128:(B0 + 2 + k) * 128],
-            vtail.at[k, e, me, RT - n:, :], l_sem.at[0, k])
-
-    def d_remote(k, p):
-        n = RT - top(k)
-        if p == 3:
-            src, chip = v_hbm.at[NL - n:, (B0 + 1 + k) * 128:(B0 + 2 + k) * 128], me
-        else:
-            chip = peers[p]
-            src = vtail.at[k, e, chip, RT - n:, :]
-        return pltpu.make_async_remote_copy(
-            src_ref=src, dst_ref=vtail.at[k, e, chip, RT - n:, :],
+    def e_local(k, g):
+        return pltpu.make_async_copy(e_ref(k, g), vtail.at[k, e, me, g * 128:, :], l_sem.at[0, k])
+
+    def d_remote(k, g, p):
+        chip = me if p == 3 else peers[p]
+        src = e_ref(k, g) if p == 3 else vtail.at[k, e, chip, g * 128:, :]
+        return pltpu.make_async_remote_copy(
+            src_ref=src, dst_ref=vtail.at[k, e, chip, g * 128:, :],
             send_sem=d_sems.at[0, k, p], recv_sem=d_sems.at[1, k, p],
             device_id=(me, 1 - e), device_id_type=MESH)
 
@@ -219,6 +210,8 @@
 
     def release(q):
         pl.semaphore_signal(vfree, inc=1, device_id=(me, 1 - e), device_id_type=MESH)
+
+    def refill(q):
         sent(q)
         pl.semaphore_wait(vfree, 1)
         fetch(q - 2)
@@ -389,10 +382,11 @@
     pl.semaphore_wait(barrier, 4)
 
     for k in reversed(range(TAIL)):
-        for p in CHIPS3:
-            e_remote(k, p).start()
-        e_local(k).start()
-        d_remote(k, 3).start()
+        g = k // 2
+        for p in CHIPS3:
+            e_remote(k, g, p).start()
+        e_local(k, g).start()
+        d_remote(k, g, 3).start()
         f_remote(k).start()
         f_local(k).start()
     for d in CHIPS4:
@@ -422,20 +416,20 @@
         def _():
             fn(q)
 
-    def corner_pass(k):
-        for p in CHIPS3:
-            e_remote(k, p).wait_recv()
-            d_remote(k, p).start()
-
-    def corner(k):
-        o = top(k)
+    def corner_pass(k, g):
+        for p in CHIPS3:
+            e_remote(k, g, p).wait_recv()
+            d_remote(k, g, p).start()
+
+    def corner(k, g):
+        o = g * 128
         n = RT - o
         free = (B0 + 1) % 4
-        e_local(k).wait()
+        e_local(k, g).wait()
         f_local(k).wait()
         f_remote(k).wait_recv()
         for p in CHIPS4:
-            d_remote(k, p).wait_recv()
+            d_remote(k, g, p).wait_recv()
         gacc[...] = jnp.zeros_like(gacc)
 
         def split_chip(d):
@@ -465,16 +459,22 @@
     prep_all(B0)
     when_own(B0, g_start)
     release(B0)
+    refill(B0)
     prep_all(B0 - 1)
     when_own(B0 - 1, g_start)
     release(B0 - 1)
+    refill(B0 - 1)
     for d in CHIPS4:
         h_local(d).wait()
-    corner_pass(TAIL - 1)
-    for k in reversed(range(TAIL)):
-        if k:
-            corner_pass(k - 1)
-        corner(k)
+    for g in reversed(range(TAIL // 2)):
+        corner_pass(2 * g + 1, g)
+
+        def pair(n):
+            @pl.when(n == 0)
+            def _():
+                corner_pass(2 * g, g)
+            corner(2 * g + 1 - n, g)
+        loop(0, 2, pair)
     for p in CHIPS3:
         x_remote(p).start()
     xT[chunk(me), NL - RT:] = xtail[:, pl.ds(pl.multiple_of(me * RT, RT), RT)]
@@ -545,6 +545,10 @@
                 g_mid(b - 2)
             t_build(b - 1)
 
+            @pl.when(b >= 4)
+            def _():
+                refill(b - 2)
+
         with_gram = jnp.logical_and(q3 >= 0, own(q3))
         m = M - lo
         base = lo * H
@@ -651,11 +655,11 @@
     for p in CHIPS3:
         x_remote(p).wait_send()
         for k in range(TAIL):
-            e_remote(k, p).wait_send()
+            e_remote(k, k // 2, p).wait_send()
     for k in range(TAIL):
         f_remote(k).wait_send()
         for p in CHIPS4:
-            d_remote(k, p).wait_send()
+            d_remote(k, k // 2, p).wait_send()
     sent(1)
     sent(0)
 

time: 1020 us -> 1000 us (0.980)
  Pallas kernels: 1000 us -> 984 us
    pallas_call x1, Pallas kernels: 1000 us -> 984 us  [local_apply(): pl.pallas_call(functools.partial(kernel, H, NB), out_shape=jax.ShapeDtype...]
where the time goes in v5:
time: 1000 us
  Pallas kernels  984 us (98%)
  local copies, waits for them, and re-layouts  17.9 us (2%)
    pallas_call x1, Pallas kernels, local_apply(): pl.pallas_call(functools.partial(kernel, H, NB), out_shape=jax.ShapeDtype...  984 us

profile of v5, /device:TPU:0, one launch (start us, length us, event | category | flops | bytes accessed | tf_op | source)
XLA Modules:
  0.0 1002.1 jit_solution(1760925421430826110)
XLA Ops:
  0.0 9.0 copy.4
  9.0 984.2 %back_transform.1 = f32[512,4096]{1,0:T(8,128)} custom-call(f32[64,128,128]{2,1,0:T(8,128)} %t_hbm.1, f32[4096,8192]{1,0:T(8,128)} %v_hbm.1, f32[128,16384]{1,0:T(8,128)} %bitcast.3), custom_call_target="tpu_custom_call" | custom-call | tf_op jit(solution)/shard_map/back_transform/pallas_call | solution.py:677
  993.2 8.9 copy.5

commit v6 on v5

--- a/solution.py
+++ b/solution.py
@@ -48,8 +48,8 @@
 
 def kernel(H, NB, t_hbm, v_hbm, z_hbm, out_hbm,
            xT, vst, vb, tst, tp, ysp, xs, wacc, wsend, wrecv, ysend, yT,
-           gacc, gsend, grecv, gown, gfull, t01s, t01r, vtail, ttail, xtail,
-           z_send, z_recv, z_loc, v_send, v_recv, v_loc, t_send, t_recv, t_loc,
+           gacc, gsend, grecv, gown, gfull, t01s, t01r, vtail, ttail, xtail, zst,
+           z_send, z_recv, z_loc, z_in, v_send, v_recv, v_loc, t_send, t_recv, t_loc,
            rs_send, rs_recv, ag_send, ag_recv, g_sems, p_send, p_recv, o_sem, e_sems, d_sems, l_sem, x_sems, vfree):
     NL = xT.shape[1]
     M = NL // H
@@ -79,9 +79,14 @@
     def own(q):
         return lax.rem(q, 2) == e
 
+    def z_load(k, p):
+        return pltpu.make_async_copy(
+            z_hbm.at[:, pl.ds(pl.multiple_of(peers[p] * NL + k * 128, 128), 128)],
+            zst.at[lax.rem(k, 4), p], z_in.at[lax.rem(k, 4), p])
+
     def z_remote(k, p):
         return pltpu.make_async_remote_copy(
-            src_ref=z_hbm.at[:, pl.ds(pl.multiple_of(peers[p] * NL + k * 128, 128), 128)],
+            src_ref=zst.at[lax.rem(k, 4), p],
             dst_ref=xT.at[chunk(me), pl.ds(pl.multiple_of(k * 128, 128), 128)],
             send_sem=z_send.at[k, p], recv_sem=z_recv.at[k, p],
             device_id=(peers[p], e), device_id_type=MESH)
@@ -149,7 +154,7 @@
 
     def e_remote(k, g, p):
         return pltpu.make_async_remote_copy(
-            src_ref=e_ref(k, g), dst_ref=vtail.at[k, e, me, g * 128:, :],
+            src_ref=vtail.at[k, e, me, g * 128:, :], dst_ref=vtail.at[k, e, me, g * 128:, :],
             send_sem=e_sems.at[0, k, p], recv_sem=e_sems.at[1, k, p],
             device_id=(peers[p], e), device_id_type=MESH)
 
@@ -158,9 +163,8 @@
 
     def d_remote(k, g, p):
         chip = me if p == 3 else peers[p]
-        src = e_ref(k, g) if p == 3 else vtail.at[k, e, chip, g * 128:, :]
-        return pltpu.make_async_remote_copy(
-            src_ref=src, dst_ref=vtail.at[k, e, chip, g * 128:, :],
+        return pltpu.make_async_remote_copy(
+            src_ref=vtail.at[k, e, chip, g * 128:, :], dst_ref=vtail.at[k, e, chip, g * 128:, :],
             send_sem=d_sems.at[0, k, p], recv_sem=d_sems.at[1, k, p],
             device_id=(me, 1 - e), device_id_type=MESH)
 
@@ -363,10 +367,20 @@
         for i, piece in enumerate(split3(yT[c])):
             ysp[i * C:(i + 1) * C, :] = piece
 
-    def z_start(k):
+    def z_stage(k):
+        @pl.when(k + 4 < ZE)
+        def _():
+            for p in CHIPS3:
+                z_remote(k + 4, p).wait_send()
+        for p in CHIPS3:
+            z_load(k, p).start()
+        z_local(k).start()
+
+    def z_go(k):
+        for p in CHIPS3:
+            z_load(k, p).wait()
         for p in CHIPS3:
             z_remote(k, p).start()
-        z_local(k).start()
 
     def z_wait(t):
         def one(k):
@@ -382,24 +396,30 @@
     pl.semaphore_wait(barrier, 4)
 
     for k in reversed(range(TAIL)):
-        g = k // 2
-        for p in CHIPS3:
-            e_remote(k, g, p).start()
-        e_local(k, g).start()
-        d_remote(k, g, 3).start()
+        e_local(k, k // 2).start()
         f_remote(k).start()
         f_local(k).start()
+    for k in reversed(range(TAIL)):
+        e_local(k, k // 2).wait()
+        for p in CHIPS3:
+            e_remote(k, k // 2, p).start()
+        d_remote(k, k // 2, 3).start()
     for d in CHIPS4:
         h_local(d).start()
     fetch(B0)
     fetch(B0 - 1)
 
     def z_first(n):
-        z_start(ZE - 1 - n)
+        z_stage(ZE - 1 - n)
+
+    def z_second(n):
+        z_go(ZE - 1 - n)
     ZS = (B0 - 1) // TB * ZP
     late = TB - 1 - (B0 - 1) % TB - 1
     step = TB // ZP
-    loop(0, ZE - ZS + (late + step - 1) // step, z_first)
+    early = ZE - ZS + (late + step - 1) // step
+    loop(0, early, z_first)
+    loop(0, early, z_second)
 
     def prep_all(q):
         arrived(q)
@@ -425,7 +445,6 @@
         o = g * 128
         n = RT - o
         free = (B0 + 1) % 4
-        e_local(k, g).wait()
         f_local(k).wait()
         f_remote(k).wait_recv()
         for p in CHIPS4:
@@ -521,17 +540,19 @@
         lo = (b - 1) // TB
         q3 = b - 3
 
+        back = TB * (lo + 1) - 1 - b
+        z_now = jnp.logical_and(jnp.logical_and(lo >= 1, back >= 0), lax.rem(back, TB // ZP) == 0)
+        z_piece = lo * ZP - 1 - back // (TB // ZP)
+
         @pl.when(c == 0)
         def _():
             @pl.when(lax.rem(b, TB) == 0)
             def _():
                 z_wait(lo)
 
-            back = TB * (lo + 1) - 1 - b
-
-            @pl.when(jnp.logical_and(jnp.logical_and(lo >= 1, back >= 0), lax.rem(back, TB // ZP) == 0))
-            def _():
-                z_start(lo * ZP - 1 - back // (TB // ZP))
+            @pl.when(z_now)
+            def _():
+                z_stage(z_piece)
 
             @pl.when(q3 >= 0)
             def _():
@@ -540,6 +561,10 @@
 
         @pl.when(c == 1)
         def _():
+            @pl.when(z_now)
+            def _():
+                z_go(z_piece)
+
             @pl.when(jnp.logical_and(own(b - 2), b >= 2))
             def _():
                 g_mid(b - 2)
@@ -651,7 +676,7 @@
     def z_sent(k):
         for p in CHIPS3:
             z_remote(k, p).wait_send()
-    loop(0, ZE, z_sent)
+    loop(0, min(4, ZE), z_sent)
     for p in CHIPS3:
         x_remote(p).wait_send()
         for k in range(TAIL):
@@ -702,7 +727,8 @@
                 vmem((TAIL, 2, 4, 64 * TAIL, 128), F32),
                 vmem((TAIL, 2, 128, 128), F32),
                 vmem((C, 4 * 64 * TAIL), F32),
-                dma((NL // 128, 3)), dma((NL // 128, 3)), dma((NL // 128,)),
+                vmem((4, 3, C, 128), F32),
+                dma((NL // 128, 3)), dma((NL // 128, 3)), dma((NL // 128,)), dma((4, 3)),
                 *[dma((2, tiles))] * 3, *[dma((4,))] * 3,
                 *[dma((4, 3))] * 5, dma((2,)), dma((2,)), dma((4,)),
                 dma((2, TAIL, 3)), dma((2, TAIL, 5)), dma((3, max(TAIL, 4))), dma((2, 3)),

time: 1000 us -> 1010 us (1.010)
  no operation moved by 1% of the time
where the time goes in v6:
time: 1010 us
  Pallas kernels  988 us (98%)
  local copies, waits for them, and re-layouts  17.9 us (2%)
    pallas_call x1, Pallas kernels, local_apply(): pl.pallas_call(functools.partial(kernel, H, NB), out_shape=jax.ShapeDtype...  988 us

profile of v6, /device:TPU:0, one launch (start us, length us, event | category | flops | bytes accessed | tf_op | source)
XLA Modules:
  0.0 1006.4 jit_solution(17614650211462078449)
XLA Ops:
  0.0 9.0 copy.4
  9.0 988.4 %back_transform.1 = f32[512,4096]{1,0:T(8,128)} custom-call(f32[64,128,128]{2,1,0:T(8,128)} %t_hbm.1, f32[4096,8192]{1,0:T(8,128)} %v_hbm.1, f32[128,16384]{1,0:T(8,128)} %bitcast.3), custom_call_target="tpu_custom_call" | custom-call | tf_op jit(solution)/shard_map/back_transform/pallas_call | solution.py:702
  997.4 8.9 copy.5
